TPU v7x, 256 devices: a whole 4x4x8 slice. The times are simulated.
256 devices in a mesh: dom: 4 (over x_lo, core), orient: 64 (over x_hi, y, z).
Axes of the slice: x: 4 (x_hi: 2, x_lo: 2; x = x_hi * 2 + x_lo), y: 4, z: 8, core: 2. Of those that a mesh axis runs over, the one named last changes fastest.
Arguments:
- particles: bfloat16 [2048, 2, 8192], P(('dom', 'orient')), may hold values from -48 to 48
- templates: bfloat16 [16384, 2, 8192], P('orient'), may hold values from -6 to 6
- tilt_low: int32 [2048], P(('dom', 'orient')), may hold values from 0 to 23
- tilt_high: int32 [2048], P(('dom', 'orient')), may hold values from 40 to 63
Outputs:
- updated: float32 [16384, 2, 8192], P('orient', None, 'dom')
- log_evidence: float32 [2048], P('dom')
All inputs are finite; a program needn't handle non-finite values.
Results may differ from a plain program's by a relative error of at most 0.0045.
Values may be sent and summed in bfloat16 or wider, within the bound.
A program may use at most 192 MiB of HBM per device.

v0:
```python
import math

import jax
import jax.numpy as jnp
from jax import lax
from jax.sharding import PartitionSpec as P

NBIN = 64


def side_by_side(arrays, axis, dim, along):
    widths = [math.prod(a.shape[along:]) for a in arrays]
    both = jnp.concatenate(
        [a.reshape(*a.shape[:along], w) for a, w in zip(arrays, widths)], axis=along
    )
    filled = lax.all_gather(both, axis, axis=dim, tiled=True)
    pieces = jnp.split(filled, [sum(widths[:k]) for k in range(1, len(widths))], axis=along)
    return tuple(
        (b.reshape(*filled.shape[:along], *a.shape[along:]) for a, b in zip(arrays, pieces))
    )


def from_everyone(x, axis):
    copies = jnp.broadcast_to(x, (lax.axis_size(axis), *x.shape))
    return lax.all_to_all(copies, axis, split_axis=0, concat_axis=0, tiled=True)


def collected_together(x, axis):
    leaves = jax.tree.leaves(x)
    sequence = sorted(range(len(leaves)), key=lambda k: -leaves[k].size)
    width = (1, *leaves[sequence[0]].shape)[-1]
    lines = [
        jnp.pad(leaves[k].reshape(-1), (0, -leaves[k].size % width)).reshape(-1, width)
        for k in sequence
    ]
    both, at, found = (from_everyone(jnp.concatenate(lines), axis), 0, {})
    for k, line in zip(sequence, lines):
        slab = both[:, at : at + len(line)].reshape(len(both), -1)
        found[k] = slab[:, : leaves[k].size].reshape(-1, *leaves[k].shape)
        at += len(line)
    numbers = iter(range(len(leaves)))
    return jax.tree.map(lambda _: found[next(numbers)], x)


def folded_in_pairs(pieces, combine):
    while len(jax.tree.leaves(pieces)[0]) > 1:
        pieces = jax.vmap(combine)(
            *(jax.tree.map(lambda part: part[side::2], pieces) for side in (0, 1))
        )
    return jax.tree.map(lambda part: part[0], pieces)


def merged(x, axis, combine):
    pieces = collected_together(x, axis)
    return folded_in_pairs(pieces, combine)


def over_copies(x, axis):
    everything = from_everyone(x, axis)
    return jnp.sum(everything.astype(jnp.float32), axis=0)


def bin_index(positions):
    return positions * 37 % NBIN


def combine_stats(one_side, other_side):
    joined_peak = jnp.maximum(one_side[0], other_side[0])
    joined_mass = one_side[1] * jnp.exp(one_side[0] - joined_peak) + other_side[1] * jnp.exp(
        other_side[0] - joined_peak
    )
    return (joined_peak, joined_mass)


def on_device(particles, templates, tilt_low, tilt_high):
    bounds = jnp.stack([tilt_low, tilt_high], axis=1).astype(jnp.bfloat16)
    gathered, bound_rows = side_by_side((particles, bounds), "orient", 0, 2)
    lower_bin = bound_rows[:, 0].astype(jnp.int32)
    upper_bin = bound_rows[:, 1].astype(jnp.int32)
    group_rows = gathered.shape[0]
    band_size = gathered.shape[2]
    local_refs = templates.shape[0]
    inverse_temp = 3.0 / math.sqrt(band_size)
    binned = bin_index(jnp.arange(band_size, dtype=jnp.int32))
    observed = (
        (lower_bin[:, None] <= binned[None, :]) & (binned[None, :] < upper_bin[:, None])
    ).astype(jnp.bfloat16)
    masked = gathered * observed[:, None, :]
    flat_rows = masked.reshape(group_rows, 2 * band_size)
    template_flat = templates.reshape(local_refs, 2 * band_size)
    correlation = lax.dot_general(
        flat_rows, template_flat, (((1,), (1,)), ((), ())), preferred_element_type=jnp.float32
    )
    residue_mask = observed[:, :NBIN]
    real_part = templates[:, 0, :].astype(jnp.float32)
    imag_part = templates[:, 1, :].astype(jnp.float32)
    power = real_part * real_part + imag_part * imag_part
    residue_power = jnp.sum(power.reshape(local_refs, band_size // NBIN, NBIN), axis=1)
    penalty = jnp.dot(
        residue_mask.astype(jnp.float32), residue_power.T, precision=lax.Precision.HIGHEST
    )
    scores = inverse_temp * (correlation - 0.5 * penalty)
    local_peak = jnp.max(scores, axis=1)
    local_mass = jnp.sum(jnp.exp(scores - local_peak[:, None]), axis=1)
    peak_score, total_mass = merged((local_peak, local_mass), "orient", combine_stats)
    log_evidence = peak_score + jnp.log(total_mass)
    weights = jnp.exp(scores - log_evidence[:, None]).astype(jnp.bfloat16)
    numerator = lax.dot_general(
        weights, flat_rows, (((0,), (0,)), ((), ())), preferred_element_type=jnp.float32
    )
    numerator = numerator.reshape(local_refs, 2, band_size)
    dom_count = lax.axis_size("dom")
    slice_width = band_size // dom_count
    slice_start = lax.axis_index("dom") * slice_width
    previous = lax.dynamic_slice_in_dim(templates, slice_start, slice_width, 2).astype(jnp.float32)
    summed_num = lax.psum_scatter(
        numerator.astype(jnp.bfloat16), "dom", scatter_dimension=2, tiled=True
    ).astype(jnp.float32)
    residue_weights = lax.dot_general(
        weights, residue_mask, (((0,), (0,)), ((), ())), preferred_element_type=jnp.float32
    )
    residue_weights = over_copies(residue_weights.astype(jnp.bfloat16), "dom").astype(jnp.float32)
    tiled_weights = jnp.tile(residue_weights, (1, band_size // NBIN))
    summed_den = lax.dynamic_slice_in_dim(tiled_weights, slice_start, slice_width, 1)[:, None, :]
    updated = (summed_num + previous) / (summed_den + 1.0)
    return (updated, log_evidence)


def solution(mesh):
    in_specs = (
        P(("dom", "orient"), None, None),
        P("orient", None, None),
        P(("dom", "orient")),
        P(("dom", "orient")),
    )
    out_specs = (P("orient", None, "dom"), P("dom"))
    return jax.shard_map(
        on_device, mesh=mesh, in_specs=in_specs, out_specs=out_specs, check_vma=False
    )
```

profile of v0, /device:TPU:1, one launch (start us, length us, event | category | flops | bytes accessed | tf_op | source)
XLA Modules:
  0.0 442.9 jit_solution(12081234740999426776)
XLA Ops:
  7.2 0.7 convert_bitcast_fusion
  7.9 0.1 copy.26
  8.0 1.9 pad_maximum_fusion
  9.9 26.6 %fusion.18 = (bf16[256,1,8192]{2,1,0:T(2,128)(2,1)}, bf16[256,1,8192]{2,1,0:T(2,128)(2,1)}) fusion(bf16[256,2,8192]{2,1,0:T(2,128)(2,1)} %param.5), kind=kLoop, calls=%fused_computation.48 | loop fusion | bytes 16777216 | tf_op jit(solution)/shard_map/slice | solution.py:95
  36.5 17.3 %copy.38 = bf16[256,1,8192]{0,2,1:T(8,128)(2,1)} copy(bf16[256,1,8192]{2,1,0:T(2,128)(2,1)} %get-tuple-element.18) | data formatting | bytes 8388608
  53.8 17.2 %copy.39 = bf16[256,1,8192]{0,2,1:T(8,128)(2,1)} copy(bf16[256,1,8192]{2,1,0:T(2,128)(2,1)} %get-tuple-element.19) | data formatting | bytes 8388608
  71.1 8.1 %multiply_add_fusion = f32[256,1,8192]{0,2,1:T(8,128)} fusion(bf16[256,1,8192]{0,2,1:T(8,128)(2,1)} %copy.39, bf16[256,1,8192]{0,2,1:T(8,128)(2,1)} %copy.38), kind=kLoop, calls=%fused_computation.5 | loop fusion | flops 10485760 | bytes 16777216 | tf_op jit(solution)/shard_map/add | solution.py:97
  79.2 3.9 reduce_sum.27
  83.0 142.4 %all-gather.2.cloned.1.call-done = bf16[512,2,8193]{2,1,0:T(2,128)(2,1)} async-done(((bf16[8,2,8193]{2,1,0:T(2,128)(2,1)}), bf16[512,2,8193]{2,1,0:T(2,128)(2,1)}) %all-gather.2.cloned.1.call-update) | async-done | bytes 16779280 | tf_op jit(solution)/shard_map/all_gather | solution.py:16
  225.4 1.1 split.9
  226.5 0.1 copy.27
  226.7 4.9 %compare_and_fusion = (pred[512,8192]{1,0:T(32,128)(4,1)}, bf16[512,8192]{1,0:T(8,128)(2,1)S(1)}) fusion(s32[8192]{0:T(1024)S(1)} %add_select_fusion, s32[512]{0:T(512)S(1)} %bitcast.45, s32[512]{0:T(512)S(1)} %bitcast.44), kind=kLoop, calls=%fused_computation.3 | loop fusion | flops 16777216 | bytes 12619776 | tf_op jit(solution)/shard_map/and | solution.py:86
  231.6 22.4 %slice_multiply_fusion = bf16[512,2,8192]{2,1,0:T(2,128)(2,1)} fusion(bf16[512,2,8193]{2,1,0:T(2,128)(2,1)} %all-gather.2.cloned.1.call-done, bf16[512,8192]{1,0:T(8,128)(2,1)S(1)} %get-tuple-element.23), kind=kLoop, calls=%fused_computation | loop fusion | flops 8388608 | bytes 41943040 | tf_op jit(solution)/shard_map/mul | solution.py:88
  254.0 26.5 %fusion.4 = f32[512,256]{0,1:T(8,128)S(1)} fusion(bf16[512,2,8192]{2,1,0:T(2,128)(2,1)} %slice_multiply_fusion, bf16[256,2,8192]{2,1,0:T(2,128)(2,1)} %param.5), kind=kOutput, calls=%fused_computation.11 | convolution fusion | flops 4294967296 | bytes 25690112 | tf_op jit(solution)/shard_map/dot_general | solution.py:91
  280.5 1.2 fusion.20
  281.8 0.1 exponential_reduce_fusion
  281.9 0.8 broadcast_in_dim.4
  282.7 7.5 %all-to-all-start = ((f32[64,2,512]{2,1,0:T(2,128)}), f32[64,2,512]{2,1,0:T(2,128)S(1)}, u32[]{:S(2)}, u32[]{:S(2)}) async-start(f32[64,2,512]{2,1,0:T(2,128)} %broadcast_in_dim.4), calls=%async_computation | async-start | bytes 524288 | tf_op jit(solution)/shard_map/all_to_all | solution.py:25
  290.2 18.5 %copy.41 = bf16[64,8,2,8192]{3,1,2,0:T(8,128)(2,1)} copy(bf16[64,8,2,8192]{3,2,1,0:T(2,128)(2,1)} %bitcast.31) | data formatting | bytes 33554432
  308.8 22.4 %copy.33 = bf16[16384,512]{1,0:T(8,128)(2,1)} copy(bf16[16384,512]{0,1:T(8,128)(2,1)} %bitcast.32) | data formatting | bytes 33554432 | tf_op jit(solution)/shard_map/dot_general | solution.py:108
  331.1 0.2 fusion.19
  332.0 10.2 %convolution_convert_fusion = bf16[256,2,8192]{2,0,1:T(8,128)(2,1)} fusion(bf16[2,8192,512]{2,1,0:T(8,128)(2,1)} %bitcast.30, f32[512,256]{0,1:T(8,128)S(1)} %get-tuple-element.27, f32[512]{0:T(512)S(1)} %bitcast.39), kind=kOutput, calls=%fused_computation.4 | convolution fusion | flops 4299423744 | bytes 25692160 | tf_op jit(solution)/shard_map/dot_general | solution.py:108
  342.3 1.0 convolution_convert_fusion.1
  343.3 0.7 broadcast_in_dim.5
  344.0 5.0 %all-to-all-start.1 = ((bf16[4,256,64]{1,2,0:T(8,128)(2,1)}), bf16[4,256,64]{1,2,0:T(8,128)(2,1)S(1)}, u32[]{:S(2)}, u32[]{:S(2)}) async-start(bf16[4,256,64]{1,2,0:T(8,128)(2,1)} %broadcast_in_dim.5), calls=%async_computation.2 | async-start | bytes 262144 | tf_op jit(solution)/shard_map/all_to_all | solution.py:25
  349.0 12.5 %copy.29 = bf16[256,2,8192]{2,0,1:T(8,128)(2,1)} copy(bf16[256,2,8192]{2,1,0:T(2,128)(2,1)} %param.5) | data formatting | bytes 16777216 | tf_op args[1]
  361.5 1.0 tile.4
  362.6 0.1 dynamic-slice_add_fusion
  362.7 1.8 copy.35
  364.5 62.6 %reduce-scatter.2.cloned.1.call-done = bf16[256,2,2048]{2,0,1:T(8,128)(2,1)} async-done(((bf16[256,2,8192]{2,0,1:T(8,128)(2,1)}), bf16[256,2,2048]{2,0,1:T(8,128)(2,1)}) %reduce-scatter.2.cloned.1.call-update) | async-done | bytes 2097168 | tf_op jit(solution)/shard_map/reduce_scatter | solution.py:116
  427.1 3.8 add_divide_fusion
  430.9 5.2 %copy.36 = f32[256,2,2048]{2,1,0:T(2,128)} copy(f32[256,2,2048]{2,0,1:T(8,128)S(1)} %add_divide_fusion) | data formatting | bytes 8388608
  (41 shorter events, 0.8 us)
Async XLA Ops:
  7.2 218.2 %all-gather.2.cloned.1.call-start = ((), (), s32[]{:S(2)}) async-start(), calls=%async_computation.3 | async-start | bytes 17305600 | tf_op jit(solution)/shard_map/all_gather | solution.py:16
  282.7 48.5 %all-to-all-start = ((f32[64,2,512]{2,1,0:T(2,128)}), f32[64,2,512]{2,1,0:T(2,128)S(1)}, u32[]{:S(2)}, u32[]{:S(2)}) async-start(f32[64,2,512]{2,1,0:T(2,128)} %broadcast_in_dim.4), calls=%async_computation | async-start | bytes 524288 | tf_op jit(solution)/shard_map/all_to_all | solution.py:25
  290.2 136.9 %reduce-scatter.2.cloned.1.call-start = ((), (), s32[]{:S(2)}) async-start(), calls=%async_computation.4 | async-start | bytes 10485760 | tf_op jit(solution)/shard_map/reduce_scatter | solution.py:116
  332.0 10.3 %copy-start = (f32[1,512]{1,0:T(1,128)}, f32[1,512]{1,0:T(1,128)S(1)}, u32[]{:S(2)}) copy-start(f32[1,512]{1,0:T(1,128)S(1)} %log_add_fusion) | copy-start | bytes 6148
  344.0 17.5 %all-to-all-start.1 = ((bf16[4,256,64]{1,2,0:T(8,128)(2,1)}), bf16[4,256,64]{1,2,0:T(8,128)(2,1)S(1)}, u32[]{:S(2)}, u32[]{:S(2)}) async-start(bf16[4,256,64]{1,2,0:T(8,128)(2,1)} %broadcast_in_dim.5), calls=%async_computation.2 | async-start | bytes 262144 | tf_op jit(solution)/shard_map/all_to_all | solution.py:25
Sparse Core Ops, SparseCore 0:
  11.7 213.6 all-gather.1
  342.4 84.6 reduce-scatter.1
where the time goes:
time: 445 us; the launch traced here: 443 us
  waiting for transfers between devices  205 us (46%)
  local copies, waits for them, and re-layouts  126 us (28%)
  other arithmetic  46 us (10%)
  matrix products  39 us (9%)
  between operations  14.2 us (3%)
  starting transfers between devices  12.6 us (3%)
    all_gather x1, waiting for transfers between devices, side_by_side(): filled = lax.all_gather(both, axis, axis=dim, tiled=True)  142 us
    unnamed x9, local copies, waits for them, and re-layouts  70.8 us
    reduce_scatter x1, waiting for transfers between devices, on_device(): lax.psum_scatter(numerator.astype(jnp.bfloat16), 'dom', scatter_dimension...  62.6 us
    slice x1, local copies, waits for them, and re-layouts, on_device(): real_part = templates[:, 0, :].astype(jnp.float32)  26.6 us
    dot_general x1, matrix products, on_device(): lax.dot_general(flat_rows, template_flat, (((1,), (1,)), ((), ())), prefe...  26.5 us
    mul x1, other arithmetic, on_device(): masked = gathered * observed[:, None, :]  22.4 us
    dot_general x1, local copies, waits for them, and re-layouts, on_device(): lax.dot_general(weights, flat_rows, (((0,), (0,)), ((), ())), preferred_e...  22.4 us
    all_to_all x2, starting transfers between devices, from_everyone(): return lax.all_to_all(copies, axis, split_axis=0, concat_axis=0, tiled=True)  12.5 us
  transfers between devices with their start and end apart: 4, of which 2 were waited for; matrix products, arithmetic and copies ran while one was open for 30% of the time, Pallas kernels for 0%

commit v1 on v0

v1 whole, which is shorter than its diff:
```python
import functools
import math

import jax
import jax.numpy as jnp
from jax import lax
from jax.experimental import pallas as pl
from jax.experimental.pallas import tpu as pltpu
from jax.sharding import PartitionSpec as P

NBIN = 64
NX, NY, NZ, ND = 2, 4, 8, 4
LANES = 128
RING = (0, 7, 1, 6, 2, 5, 3, 4)
BW = {"x": 23.3, "y+": 46.6, "y-": 46.6, "z+": 46.6, "z-": 46.6}
LATENCY = 2.0


def moved(unit, link):
    x, z, y = unit
    if link == "x":
        return 1 - x, z, y
    step = -1 if link[1] == "+" else 1
    return (x, (z + step) % NZ, y) if link[0] == "z" else (x, z, (y + step) % NY)


def plan(cols, first_a, second_a, x_cols):
    sends = []

    def add(link, unit, part, lo, hi, rank):
        sends.append(
            dict(link=link, unit=unit, part=part, lo=lo, hi=hi, rank=rank, lands=moved(unit, link))
        )

    add("x", (0, 0, 0), "F", 0, cols, 0)
    for x in (0, 1):
        cut, end = (first_a, cols) if x == 0 else (second_a, cols - x_cols)
        plus = x == 0
        add("y+", (x, 0, 0), "A", 0, cut, 0)
        add("y-", (x, 0, 0), "A", 0, cut, 0)
        add(*(("y+", (x, 0, 3)) if plus else ("y-", (x, 0, 1))), "A", 0, cut, 0)
        for k in range(4):
            if k < 3 or plus:
                add("z+", (x, -k % NZ, 0), "B", cut, end, 1)
            if k < 3 or not plus:
                add("z-", (x, k, 0), "B", cut, end, 1)
        for k in range(4):
            for y in (0, 3, 1, 2):
                if k < 3 or y in (0, 3):
                    add("z+", (x, -k % NZ, y), "A", 0, cut, 2)
                if k < 3 or y in (1, 2):
                    add("z-", (x, k, y), "A", 0, cut, 2)
        for n, z in enumerate(RING):
            add("y+", (x, z, 0), "B", cut, end, 2)
            add("y-", (x, z, 0), "B", cut, end, 2)
            add(*(("y+", (x, z, 3)) if n % 2 == 0 else ("y-", (x, z, 1))), "B", cut, end, 2)
        if x == 0 and x_cols:
            for z in RING:
                for y in (0, 3, 1, 2):
                    if (z, y) != (0, 0):
                        add("x", (0, z, y), "X", cols - x_cols, cols, 3)
    for number, s in enumerate(sends):
        s["id"] = number
    arrives = {(s["lands"], s["part"]): s["id"] for s in sends}
    for s in sends:
        part = "B" if s["part"] == "X" else s["part"]
        own = {(0, 0, 0): None, (1, 0, 0): 0}
        s["needs"] = own[s["unit"]] if s["unit"] in own else arrives[s["unit"], part]

    free, landed, left, events = dict.fromkeys(BW, 0.0), {None: 0.0}, list(sends), []
    while left:
        able = [s for s in left if s["needs"] in landed]
        key = lambda s: (
            max(landed[s["needs"]], free[s["link"]]), s["unit"][0], s["rank"], s["id"]
        )
        s = min(able, key=key)
        start = max(landed[s["needs"]], free[s["link"]])
        free[s["link"]] = start + (s["hi"] - s["lo"]) * 8.192 / BW[s["link"]]
        landed[s["id"]] = free[s["link"]] + LATENCY
        events.append(s)
        left.remove(s)
    when, latest = {}, dict.fromkeys(BW, 0.0)
    for s in events:
        latest[s["link"]] = max(latest[s["link"]], landed[s["needs"]])
        when[s["id"]] = latest[s["link"]]
    batches = []
    for x in (0, 1):
        for z in range(NZ):
            wanted = [
                arrives[(x, z, y), part]
                for y in range(NY)
                for part in "FABX"
                if ((x, z, y), part) in arrives
            ]
            batches.append((max(landed[w] for w in wanted), x, z, wanted))
    batches.sort()
    order = sorted(events, key=lambda s: when[s["id"]])
    segments, at = [], 0
    for done, _, _, wanted in batches:
        stop = at
        while stop < len(order) and when[order[stop]["id"]] <= done:
            stop += 1
        segments.append((order[at:stop], wanted))
        at = stop
    assert at == len(order)
    return sends, segments, [(x, z) for _, x, z, _ in batches]


def table(values, index):
    total = jnp.int32(0)
    for n, v in enumerate(values):
        if v:
            total = total + jnp.where(index == n, v, 0)
    return total


def em_kernel(
    schedule, temp, block, temps, out, lz_out,
    rows, scores, parts, weights, evid, stat, stat_z, stat_q, power, inverse, local_sem,
    send_sem, recv_sem, ps_send, ps_recv, zs_send, zs_recv, qs_send, qs_recv,
    w_send, w_recv, l_send, l_recv,
):
    sends, segments, batches = schedule
    dom, orient = lax.axis_index("dom"), lax.axis_index("orient")
    x0, y0, z0 = orient // (NY * NZ), (orient // NZ) % NY, orient % NZ
    q0 = x0 * NY + y0
    width = temps.shape[1]
    refs = temps.shape[0]

    def at(x, y, z):
        return {"orient": (x * NY + y) * NZ + z}

    def at_q(q):
        return {"orient": q * NZ + z0}

    target = {
        "x": at(1 - x0, y0, z0),
        "y+": at(x0, (y0 + 1) % NY, z0),
        "y-": at(x0, (y0 + NY - 1) % NY, z0),
        "z+": at(x0, y0, (z0 + 1) % NZ),
        "z-": at(x0, y0, (z0 + NZ - 1) % NZ),
    }
    z_peer = [at(x0, y0, (z0 + k) % NZ) for k in range(NZ)]
    q_peer = [at_q((q0 + k) % (NX * NY)) for k in range(NX * NY)]
    d_peer = [{"dom": (dom + k) % ND} for k in range(ND)]
    chip_peer = {"dom": dom + 1 - 2 * (dom % 2)}
    side_peer = {"dom": (dom + 2) % ND}
    chip_dom = dom + 1 - 2 * (dom % 2)
    side_dom = (dom + 2) % ND

    barrier = pltpu.get_barrier_semaphore()
    greeted = z_peer[1:] + q_peer[1:] + d_peer[1:]
    for peer in greeted:
        pl.semaphore_signal(barrier, inc=1, device_id=peer, device_id_type=pl.DeviceIdType.MESH)
    pl.semaphore_wait(barrier, len(greeted))

    z_at = [((z0 + k) % NZ % ND) * 512 + ((z0 + k) % NZ // ND) * 128 for k in range(NZ)]
    y_at = [((y0 + k) % NY) * 32 for k in range(NY)]
    x_at = [x0 * 256, (1 - x0) * 256]

    def unit_rows(unit):
        x, z, y = unit
        return pl.ds(pl.multiple_of(x_at[x] + z_at[z] + y_at[y], 32), 32)

    def remote(src, dst, ssem, rsem, peer):
        return pltpu.make_async_remote_copy(
            src_ref=src, dst_ref=dst, send_sem=ssem, recv_sem=rsem,
            device_id=peer, device_id_type=pl.DeviceIdType.MESH,
        )

    def copy_of(s, unit):
        columns = pl.ds(s["lo"] * LANES, (s["hi"] - s["lo"]) * LANES)
        place = rows.at[unit_rows(unit), columns]
        src = block.at[:, columns] if unit == (0, 0, 0) else place
        return remote(
            src, place, send_sem.at[s["id"]], recv_sem.at[s["id"]], target[s["link"]]
        )

    own = pltpu.make_async_copy(block, rows.at[unit_rows((0, 0, 0)), :], local_sem)
    own.start()

    heard = set()

    def hear(number):
        if number is not None and number not in heard:
            heard.add(number)
            copy_of(sends[number], sends[number]["lands"]).wait_recv()

    def partial_copy(pos):
        owner, part = pos // ND, pos % ND
        rel = (dom - owner + ND) % ND - 1
        return remote(
            scores.at[pos], parts.at[jnp.maximum(rel, 0), part], ps_send.at[pos],
            ps_recv.at[jnp.maximum(rel, 0), part], {"dom": owner},
        )

    def phase_body(phase, carry):
        for n, (issue, wanted) in enumerate(segments):

            @pl.when(phase == n)
            def _(n=n, issue=issue, wanted=wanted):
                for s in issue:
                    hear(s["needs"])
                    copy_of(s, s["unit"]).start()
                for w in wanted:
                    hear(w)
                if n == 0:
                    own.wait()
                    total = jnp.zeros((refs, LANES), jnp.float32)
                    for c in range(width // LANES):
                        piece = temps[:, c * LANES : (c + 1) * LANES].astype(jnp.float32)
                        total = total + piece * piece
                    total = 0.5 * total
                    for c in range(3):
                        head = total.astype(jnp.bfloat16)
                        power[c] = head
                        total = total - head.astype(jnp.float32)

        bx = table([b[0] for b in batches], phase)
        bz = (z0 + table([b[1] for b in batches], phase)) % NZ
        bx = (x0 + bx) % NX
        pos = (bz % ND) * ND + bx * 2 + bz // ND
        here = pl.ds(pl.multiple_of(pos * LANES, LANES), LANES)
        nt = (((1,), (1,)), ((), ()))
        mask = rows[here, width : width + LANES]
        penalty = lax.dot_general(power[2], mask, nt, preferred_element_type=jnp.float32)
        for c in (1, 0):
            penalty = penalty + lax.dot_general(
                power[c], mask, nt, preferred_element_type=jnp.float32
            )
        corr = lax.dot_general(
            temps[...], rows[here, :width], nt, preferred_element_type=jnp.float32
        )
        scores[pos] = corr - penalty

        @pl.when(pos // ND != dom)
        def _():
            partial_copy(pos).start()

        return carry

    lax.fori_loop(0, len(segments), phase_body, 0)

    peaks, masses = [], []
    for part in range(ND):
        mine = dom * ND + part
        total = scores[mine]
        for rel in range(ND - 1):
            remote(
                scores.at[mine], parts.at[rel, part], ps_send.at[mine], ps_recv.at[rel, part],
                d_peer[1],
            ).wait_recv()
            total = total + parts[rel, part]
        total = total * temp
        parts[0, part] = total
        peak = jnp.max(total, axis=0, keepdims=True)
        peaks.append(peak)
        masses.append(jnp.sum(jnp.exp(total - peak), axis=0, keepdims=True))
    stat[...] = jnp.concatenate(peaks + masses, axis=0)

    def merge(slots, index, peers, ssem, rsem):
        copies = [
            remote(stat, slots.at[index], ssem.at[k], rsem.at[k], peers[k])
            for k in range(1, len(peers))
        ]
        for c in copies:
            c.start()
        own_stat = stat[...]
        slots[index] = own_stat
        for k, c in enumerate(copies):
            src = (index + 2 * len(peers) - (k + 1)) % len(peers)
            remote(stat, slots.at[src], ssem.at[k + 1], rsem.at[k + 1], peers[k + 1]).wait_recv()
        both = slots[...]
        peak = jnp.max(both[:, :ND], axis=0)
        mass = jnp.sum(both[:, ND:] * jnp.exp(both[:, :ND] - peak[None]), axis=0)
        for c in copies:
            c.wait_send()
        return peak, mass

    peak, mass = merge(stat_z, z0, z_peer, zs_send, zs_recv)
    stat[...] = jnp.concatenate([peak, mass], axis=0)
    peak, mass = merge(stat_q, q0, q_peer, qs_send, qs_recv)
    log_evidence = peak + jnp.log(mass)
    evid[dom] = jnp.concatenate([log_evidence, log_evidence], axis=0)
    my_cols = pl.multiple_of(dom * 512, 512)
    for part in range(ND):
        w = jnp.exp(parts[0, part] - log_evidence[part : part + 1])
        weights[:, pl.ds(my_cols + part * LANES, LANES)] = w.astype(jnp.bfloat16)

    def w_copy(n, owner, peer):
        ref = weights.at[:, pl.ds(pl.multiple_of(owner * 512, 512), 512)]
        return remote(ref, ref, w_send.at[n], w_recv.at[n], peer)

    def l_copy(k, owner):
        return remote(evid.at[owner], evid.at[owner], l_send.at[k], l_recv.at[k], d_peer[k])

    w_copy(0, dom, side_peer).start()
    w_copy(1, dom, chip_peer).start()
    for k in range(1, ND):
        l_copy(k, dom).start()
    w_copy(0, side_dom, side_peer).wait_recv()
    w_copy(2, side_dom, chip_peer).start()
    w_copy(1, chip_dom, chip_peer).wait_recv()
    w_copy(2, (chip_dom + 2) % ND, chip_peer).wait_recv()

    den = jnp.dot(
        weights[...], rows[:, width : width + LANES], preferred_element_type=jnp.float32
    )
    inverse[...] = 1.0 / (den + 1.0)

    def tile(j, carry):
        columns = pl.ds(pl.multiple_of(j * 256, 256), 256)
        num = jnp.dot(weights[...], rows[:, columns], preferred_element_type=jnp.float32)
        scale = inverse[...]
        out[:, columns] = (num + temps[:, columns].astype(jnp.float32)) * jnp.concatenate(
            [scale, scale], axis=1
        )
        return carry

    lax.fori_loop(0, width // 256, tile, 0)

    for k in range(1, ND):
        l_copy(k, (dom + ND - k) % ND).wait_recv()
    lz_out[...] = evid[...]
    for k in range(1, ND):
        l_copy(k, dom).wait_send()
    w_copy(0, dom, side_peer).wait_send()
    w_copy(1, dom, chip_peer).wait_send()
    w_copy(2, side_dom, chip_peer).wait_send()

    def drain(pos, carry):
        @pl.when(pos // ND != dom)
        def _():
            partial_copy(pos).wait_send()

        return carry

    lax.fori_loop(0, ND * ND, drain, 0)
    for s in sends:
        copy_of(s, s["unit"]).wait_send()


def on_device(particles, templates, tilt_low, tilt_high):
    local, _, band = particles.shape
    refs = templates.shape[0]
    quarter = band // ND
    width = 2 * quarter
    temp = 3.0 / math.sqrt(band)
    bins = jnp.arange(LANES, dtype=jnp.int32) * 37 % NBIN
    observed = (tilt_low[:, None] <= bins[None, :]) & (bins[None, :] < tilt_high[:, None])
    observed = observed.astype(jnp.bfloat16)
    masked = particles * jnp.tile(observed, (1, band // LANES))[:, None, :]
    split = jnp.transpose(masked.reshape(local, 2, ND, quarter), (2, 0, 1, 3))
    split = split.reshape(ND, local, width)
    split = jnp.concatenate(
        [split, jnp.broadcast_to(observed[None], (ND, local, LANES))], axis=2
    )
    block = lax.all_to_all(split, "dom", split_axis=0, concat_axis=0, tiled=True)
    block = block.reshape(ND * local, width + LANES)
    start = lax.axis_index("dom") * quarter
    temps = lax.dynamic_slice_in_dim(templates, start, quarter, 2).reshape(refs, width)

    schedule = plan((width + LANES) // LANES, 13, 11, 6)
    count = len(schedule[0])
    dma = pltpu.SemaphoreType.DMA
    updated, evidence = pl.pallas_call(
        functools.partial(em_kernel, schedule, temp),
        out_shape=(
            jax.ShapeDtypeStruct((refs, width), jnp.float32),
            jax.ShapeDtypeStruct((ND, 8, LANES), jnp.float32),
        ),
        in_specs=[pl.BlockSpec(memory_space=pltpu.VMEM)] * 2,
        out_specs=(pl.BlockSpec(memory_space=pltpu.VMEM),) * 2,
        scratch_shapes=[
            pltpu.VMEM((NX * NY * NZ * ND * local, width + LANES), jnp.bfloat16),
            pltpu.VMEM((ND * ND, refs, LANES), jnp.float32),
            pltpu.VMEM((ND - 1, ND, refs, LANES), jnp.float32),
            pltpu.VMEM((refs, NX * NY * NZ * ND * local), jnp.bfloat16),
            pltpu.VMEM((ND, 8, LANES), jnp.float32),
            pltpu.VMEM((8, LANES), jnp.float32),
            pltpu.VMEM((NZ, 8, LANES), jnp.float32),
            pltpu.VMEM((NX * NY, 8, LANES), jnp.float32),
            pltpu.VMEM((3, refs, LANES), jnp.bfloat16),
            pltpu.VMEM((refs, LANES), jnp.float32),
            dma(()),
            dma((count,)),
            dma((count,)),
            dma((ND * ND,)),
            dma((ND - 1, ND)),
            dma((NZ,)),
            dma((NZ,)),
            dma((NX * NY,)),
            dma((NX * NY,)),
            dma((3,)),
            dma((3,)),
            dma((ND,)),
            dma((ND,)),
        ],
        compiler_params=pltpu.CompilerParams(
            collective_id=0, has_side_effects=True, vmem_limit_bytes=60 * 1024 * 1024
        ),
    )(block, temps)
    evidence = evidence[:, :ND].reshape(ND, NX, NZ // ND, NY, ND, local)
    evidence = lax.dynamic_index_in_dim(evidence, lax.axis_index("dom"), 4, keepdims=False)
    evidence = jnp.transpose(evidence, (1, 3, 2, 0, 4)).reshape(-1)
    return updated.reshape(refs, 2, quarter), evidence


def solution(mesh):
    in_specs = (
        P(("dom", "orient"), None, None),
        P("orient", None, None),
        P(("dom", "orient")),
        P(("dom", "orient")),
    )
    out_specs = (P("orient", None, "dom"), P("dom"))
    return jax.shard_map(
        on_device, mesh=mesh, in_specs=in_specs, out_specs=out_specs, check_vma=False
    )
```

time: 445 us -> 156 us (0.35)
  waiting for transfers between devices: 205 us -> 0.01 us
  Pallas kernels: 0 us -> 131 us
  local copies, waits for them, and re-layouts: 126 us -> 14.5 us
  other arithmetic: 46 us -> 2.73 us
  matrix products: 39 us -> 0 us
  between operations: 14.2 us -> 0.7 us
  starting transfers between devices: 12.6 us -> 6.62 us
    all_gather x1 -> x0, waiting for transfers between devices: 142 us -> none  [side_by_side(): filled = lax.all_gather(both, axis, axis=dim, tiled=True)]
    pallas_call x0 -> x1, Pallas kernels: none -> 131 us  [on_device(): pl.pallas_call(functools.partial(em_kernel, schedule, temp), out_shape=(j...]
    unnamed x9 -> x3, local copies, waits for them, and re-layouts: 70.8 us -> 2.91 us
    reduce_scatter x1 -> x0, waiting for transfers between devices: 62.6 us -> none  [on_device(): lax.psum_scatter(numerator.astype(jnp.bfloat16), 'dom', scatter_dimension...]
    dot_general x4 -> x0, matrix products: 39 us -> none  [the longest x1 26.5 us: on_device(): lax.dot_general(flat_rows, template_flat, (((1,), (1,)), ((), ())), prefe...]
    slice x22 -> x1, local copies, waits for them, and re-layouts: 27.3 us -> 0.72 us  [on_device(): evidence = evidence[:, :ND].reshape(ND, NX, NZ // ND, NY, ND, local)]
    dot_general x1 -> x0, local copies, waits for them, and re-layouts: 22.4 us -> none  [on_device(): lax.dot_general(weights, flat_rows, (((0,), (0,)), ((), ())), preferred_e...]
    mul x1, other arithmetic: 22.4 us -> 1.26 us  [on_device(): masked = particles * jnp.tile(observed, (1, band // LANES))[:, None, :]]
  transfers between devices with their start and end apart: 4 -> 1, of which waited for: 2 -> 0; matrix products, arithmetic and copies ran while one was open for 30% -> 3% of each run, Pallas kernels for 0% -> 0%
where the time goes in v1:
time: 156 us
  Pallas kernels  131 us (84%)
  local copies, waits for them, and re-layouts  14.5 us (9%)
  starting transfers between devices  6.62 us (4%)
  other arithmetic  2.73 us (2%)
    pallas_call x1, Pallas kernels, on_device(): pl.pallas_call(functools.partial(em_kernel, schedule, temp), out_shape=(j...  131 us
    all_to_all x1, starting transfers between devices, on_device(): lax.all_to_all(split, 'dom', split_axis=0, concat_axis=0, tiled=True)  6.62 us
    reshape x1, local copies, waits for them, and re-layouts, on_device(): return (updated.reshape(refs, 2, quarter), evidence)  6.57 us
  transfers between devices with their start and end apart: 1, of which 0 were waited for; matrix products, arithmetic and copies ran while one was open for 3% of the time, Pallas kernels for 0%

profile of v1, /device:TPU:1, one launch (start us, length us, event | category | flops | bytes accessed | tf_op | source)
XLA Modules:
  0.0 155.6 jit_solution(1957470495332343574)
XLA Ops:
  0.6 0.7 and_convert_fusion
  1.4 1.3 broadcast_multiply_fusion
  2.7 0.2 reshape.149
  2.8 0.2 copy.7
  3.0 0.7 pad_maximum_fusion
  3.7 6.6 %all-to-all-start = ((bf16[4,8,4224]{2,1,0:T(8,128)(2,1)}), bf16[4,8,4224]{2,1,0:T(8,128)(2,1)S(1)}, u32[]{:S(2)}, u32[]{:S(2)}) async-start(bf16[4,8,4224]{2,1,0:T(8,128)(2,1)} %pad_maximum_fusion), calls=%async_computation | async-start | bytes 540672 | tf_op jit(solution)/shard_map/all_to_all | solution.py:358
  10.3 3.0 %constant_dynamic-slice_fusion.1 = bf16[256,2,2048]{2,1,0:T(2,128)(2,1)S(1)} fusion(bf16[256,2,8192]{2,1,0:T(2,128)(2,1)} %param.5, s32[]{:T(128)S(6)} %select_n.21), kind=kLoop, calls=%fused_computation.10 | loop fusion | bytes 4194308 | tf_op jit(solution)/shard_map/dynamic_slice | solution.py:361
  13.4 2.2 %copy.9 = bf16[32,8,2,2048]{3,1,2,0:T(8,128)(2,1)} copy(bf16[32,8,2,2048]{3,2,1,0:T(2,128)(2,1)S(1)} %bitcast.13) | data formatting | bytes 4194304
  15.6 0.0 all-to-all-done
  15.6 0.0 copy-start
  15.6 0.7 copy-done
  16.3 131.1 %shard_map.59 = (f32[256,4096]{1,0:T(8,128)}, f32[4,8,128]{2,1,0:T(8,128)}) custom-call(bf16[32,4224]{1,0:T(8,128)(2,1)} %bitcast.14, bf16[256,4096]{1,0:T(8,128)(2,1)} %bitcast.12), custom_call_target="tpu_custom_call" | custom-call | tf_op jit(solution)/shard_map/pallas_call | solution.py:366
  147.4 0.7 slice.3
  148.1 0.2 reshape.154
  148.4 0.7 reshape.155
  149.0 6.6 %reshape.153 = f32[256,2,2048]{2,1,0:T(2,128)} reshape(f32[256,4096]{1,0:T(8,128)} %get-tuple-element.4) | data formatting | bytes 8388608 | tf_op jit(solution)/shard_map/reshape | solution.py:406
  (5 shorter events, 0.1 us)
Async XLA Ops:
  3.7 11.9 %all-to-all-start = ((bf16[4,8,4224]{2,1,0:T(8,128)(2,1)}), bf16[4,8,4224]{2,1,0:T(8,128)(2,1)S(1)}, u32[]{:S(2)}, u32[]{:S(2)}) async-start(bf16[4,8,4224]{2,1,0:T(8,128)(2,1)} %pad_maximum_fusion), calls=%async_computation | async-start | bytes 540672 | tf_op jit(solution)/shard_map/all_to_all | solution.py:358
  15.6 0.7 copy-start

commit v2 on v1

--- a/solution.py
+++ b/solution.py
@@ -12,7 +12,7 @@
 NX, NY, NZ, ND = 2, 4, 8, 4
 LANES = 128
 RING = (0, 7, 1, 6, 2, 5, 3, 4)
-BW = {"x": 23.3, "y+": 46.6, "y-": 46.6, "z+": 46.6, "z-": 46.6}
+BW = {"x": 46.6, "y+": 46.6, "y-": 46.6, "z+": 46.6, "z-": 46.6}
 LATENCY = 2.0
 
 
@@ -115,8 +115,9 @@
 
 
 def em_kernel(
-    schedule, temp, block, temps, out, lz_out,
-    rows, scores, parts, weights, evid, stat, stat_z, stat_q, power, inverse, local_sem,
+    schedule, temp, split, templates, rows_out, temps_out, weights, lz_out,
+    pairs, temps, rows, scores, parts, evid, stat, stat_z, stat_q, power,
+    local_sem, load_sem, temps_sem, rows_sem, a_send, a_recv,
     send_sem, recv_sem, ps_send, ps_recv, zs_send, zs_recv, qs_send, qs_recv,
     w_send, w_recv, l_send, l_recv,
 ):
@@ -124,8 +125,7 @@
     dom, orient = lax.axis_index("dom"), lax.axis_index("orient")
     x0, y0, z0 = orient // (NY * NZ), (orient // NZ) % NY, orient % NZ
     q0 = x0 * NY + y0
-    width = temps.shape[1]
-    refs = temps.shape[0]
+    refs, width = temps.shape
 
     def at(x, y, z):
         return {"orient": (x * NY + y) * NZ + z}
@@ -148,10 +148,28 @@
     chip_dom = dom + 1 - 2 * (dom % 2)
     side_dom = (dom + 2) % ND
 
+    quarter = width // 2
+    load = pltpu.make_async_copy(
+        templates.at[:, :, pl.ds(pl.multiple_of(dom * quarter, quarter), quarter)],
+        pairs,
+        load_sem,
+    )
+    load.start()
+
     barrier = pltpu.get_barrier_semaphore()
-    greeted = z_peer[1:] + q_peer[1:] + d_peer[1:]
+    greeted = [z_peer[1], z_peer[NZ - 1], q_peer[NY]] + d_peer[1:]
+    greeted += [target["y+"], target["y-"]]
     for peer in greeted:
         pl.semaphore_signal(barrier, inc=1, device_id=peer, device_id_type=pl.DeviceIdType.MESH)
+    load.wait()
+
+    def relayout(i, carry):
+        r = pl.ds(pl.multiple_of(i * 16, 16), 16)
+        for c in range(2):
+            temps[r, c * quarter : (c + 1) * quarter] = pairs[r, c, :]
+        return carry
+
+    lax.fori_loop(0, refs // 16, relayout, 0)
     pl.semaphore_wait(barrier, len(greeted))
 
     z_at = [((z0 + k) % NZ % ND) * 512 + ((z0 + k) % NZ // ND) * 128 for k in range(NZ)]
@@ -171,13 +189,31 @@
     def copy_of(s, unit):
         columns = pl.ds(s["lo"] * LANES, (s["hi"] - s["lo"]) * LANES)
         place = rows.at[unit_rows(unit), columns]
-        src = block.at[:, columns] if unit == (0, 0, 0) else place
         return remote(
-            src, place, send_sem.at[s["id"]], recv_sem.at[s["id"]], target[s["link"]]
-        )
-
-    own = pltpu.make_async_copy(block, rows.at[unit_rows((0, 0, 0)), :], local_sem)
+            place, place, send_sem.at[s["id"]], recv_sem.at[s["id"]], target[s["link"]]
+        )
+
+    local = split.shape[0] // ND
+    own_row = x_at[0] + z_at[0] + y_at[0]
+
+    def a_copy(k, source, owner):
+        return remote(
+            split.at[pl.ds(pl.multiple_of(owner * local, local), local)],
+            rows.at[pl.ds(pl.multiple_of(own_row + source * local, local), local)],
+            a_send.at[k], a_recv.at[k], d_peer[k],
+        )
+
+    for k in (2, 3, 1):
+        a_copy(k, dom, (dom + k) % ND).start()
+    own = pltpu.make_async_copy(
+        split.at[pl.ds(pl.multiple_of(dom * local, local), local)],
+        rows.at[pl.ds(pl.multiple_of(own_row + dom * local, local), local)],
+        local_sem,
+    )
     own.start()
+    own.wait()
+    for k in (1, 2, 3):
+        a_copy(k, (dom + ND - k) % ND, dom).wait_recv()
 
     heard = set()
 
@@ -194,6 +230,13 @@
             ps_recv.at[jnp.maximum(rel, 0), part], {"dom": owner},
         )
 
+    def rows_copy(pos):
+        here = pl.ds(pl.multiple_of(pos * LANES, LANES), LANES)
+        return pltpu.make_async_copy(rows.at[here], rows_out.at[here], rows_sem.at[pos])
+
+    temps_copy = pltpu.make_async_copy(temps, temps_out, temps_sem)
+    temps_copy.start()
+
     def phase_body(phase, carry):
         for n, (issue, wanted) in enumerate(segments):
 
@@ -202,10 +245,7 @@
                 for s in issue:
                     hear(s["needs"])
                     copy_of(s, s["unit"]).start()
-                for w in wanted:
-                    hear(w)
                 if n == 0:
-                    own.wait()
                     total = jnp.zeros((refs, LANES), jnp.float32)
                     for c in range(width // LANES):
                         piece = temps[:, c * LANES : (c + 1) * LANES].astype(jnp.float32)
@@ -215,6 +255,8 @@
                         head = total.astype(jnp.bfloat16)
                         power[c] = head
                         total = total - head.astype(jnp.float32)
+                for w in wanted:
+                    hear(w)
 
         bx = table([b[0] for b in batches], phase)
         bz = (z0 + table([b[1] for b in batches], phase)) % NZ
@@ -237,6 +279,7 @@
         def _():
             partial_copy(pos).start()
 
+        rows_copy(pos).start()
         return carry
 
     lax.fori_loop(0, len(segments), phase_body, 0)
@@ -303,26 +346,12 @@
     w_copy(1, chip_dom, chip_peer).wait_recv()
     w_copy(2, (chip_dom + 2) % ND, chip_peer).wait_recv()
 
-    den = jnp.dot(
-        weights[...], rows[:, width : width + LANES], preferred_element_type=jnp.float32
-    )
-    inverse[...] = 1.0 / (den + 1.0)
-
-    def tile(j, carry):
-        columns = pl.ds(pl.multiple_of(j * 256, 256), 256)
-        num = jnp.dot(weights[...], rows[:, columns], preferred_element_type=jnp.float32)
-        scale = inverse[...]
-        out[:, columns] = (num + temps[:, columns].astype(jnp.float32)) * jnp.concatenate(
-            [scale, scale], axis=1
-        )
-        return carry
-
-    lax.fori_loop(0, width // 256, tile, 0)
-
     for k in range(1, ND):
         l_copy(k, (dom + ND - k) % ND).wait_recv()
     lz_out[...] = evid[...]
+    temps_copy.wait()
     for k in range(1, ND):
+        a_copy(k, dom, (dom + k) % ND).wait_send()
         l_copy(k, dom).wait_send()
     w_copy(0, dom, side_peer).wait_send()
     w_copy(1, dom, chip_peer).wait_send()
@@ -333,11 +362,24 @@
         def _():
             partial_copy(pos).wait_send()
 
+        rows_copy(pos).wait()
         return carry
 
     lax.fori_loop(0, ND * ND, drain, 0)
     for s in sends:
         copy_of(s, s["unit"]).wait_send()
+
+
+def update_kernel(weights, real, imag, mask, real_temps, imag_temps, out, inverse):
+    @pl.when(pl.program_id(0) == 0)
+    def _():
+        den = jnp.dot(weights[...], mask[...], preferred_element_type=jnp.float32)
+        inverse[...] = 1.0 / (den + 1.0)
+
+    scale = jnp.concatenate([inverse[...]] * (real.shape[1] // LANES), axis=1)
+    for c, (rows, temps) in enumerate(((real, real_temps), (imag, imag_temps))):
+        num = jnp.dot(weights[...], rows[...], preferred_element_type=jnp.float32)
+        out[:, c, :] = (num + temps[...].astype(jnp.float32)) * scale
 
 
 def on_device(particles, templates, tilt_low, tilt_high):
@@ -355,34 +397,42 @@
     split = jnp.concatenate(
         [split, jnp.broadcast_to(observed[None], (ND, local, LANES))], axis=2
     )
-    block = lax.all_to_all(split, "dom", split_axis=0, concat_axis=0, tiled=True)
-    block = block.reshape(ND * local, width + LANES)
-    start = lax.axis_index("dom") * quarter
-    temps = lax.dynamic_slice_in_dim(templates, start, quarter, 2).reshape(refs, width)
-
-    schedule = plan((width + LANES) // LANES, 13, 11, 6)
+    split = split.reshape(ND * local, width + LANES)
+    schedule = plan((width + LANES) // LANES, 13, 9, 10)
     count = len(schedule[0])
     dma = pltpu.SemaphoreType.DMA
-    updated, evidence = pl.pallas_call(
+    total_rows = NX * NY * NZ * ND * local
+    rows, temps, weights, evidence = pl.pallas_call(
         functools.partial(em_kernel, schedule, temp),
         out_shape=(
-            jax.ShapeDtypeStruct((refs, width), jnp.float32),
+            jax.ShapeDtypeStruct((total_rows, width + LANES), jnp.bfloat16),
+            jax.ShapeDtypeStruct((refs, width), jnp.bfloat16),
+            jax.ShapeDtypeStruct((refs, total_rows), jnp.bfloat16),
             jax.ShapeDtypeStruct((ND, 8, LANES), jnp.float32),
         ),
-        in_specs=[pl.BlockSpec(memory_space=pltpu.VMEM)] * 2,
-        out_specs=(pl.BlockSpec(memory_space=pltpu.VMEM),) * 2,
+        in_specs=[
+            pl.BlockSpec(memory_space=pltpu.VMEM),
+            pl.BlockSpec(memory_space=pl.ANY),
+        ],
+        out_specs=(pl.BlockSpec(memory_space=pl.ANY),) * 2
+        + (pl.BlockSpec(memory_space=pltpu.VMEM),) * 2,
         scratch_shapes=[
-            pltpu.VMEM((NX * NY * NZ * ND * local, width + LANES), jnp.bfloat16),
+            pltpu.VMEM((refs, 2, quarter), jnp.bfloat16),
+            pltpu.VMEM((refs, width), jnp.bfloat16),
+            pltpu.VMEM((total_rows, width + LANES), jnp.bfloat16),
             pltpu.VMEM((ND * ND, refs, LANES), jnp.float32),
             pltpu.VMEM((ND - 1, ND, refs, LANES), jnp.float32),
-            pltpu.VMEM((refs, NX * NY * NZ * ND * local), jnp.bfloat16),
             pltpu.VMEM((ND, 8, LANES), jnp.float32),
             pltpu.VMEM((8, LANES), jnp.float32),
             pltpu.VMEM((NZ, 8, LANES), jnp.float32),
             pltpu.VMEM((NX * NY, 8, LANES), jnp.float32),
             pltpu.VMEM((3, refs, LANES), jnp.bfloat16),
-            pltpu.VMEM((refs, LANES), jnp.float32),
             dma(()),
+            dma(()),
+            dma(()),
+            dma((ND * ND,)),
+            dma((ND,)),
+            dma((ND,)),
             dma((count,)),
             dma((count,)),
             dma((ND * ND,)),
@@ -399,11 +449,29 @@
         compiler_params=pltpu.CompilerParams(
             collective_id=0, has_side_effects=True, vmem_limit_bytes=60 * 1024 * 1024
         ),
-    )(block, temps)
+    )(split, templates)
+    tile = 256
+    steps = quarter // tile
+    updated = pl.pallas_call(
+        update_kernel,
+        out_shape=jax.ShapeDtypeStruct((refs, 2, quarter), jnp.float32),
+        grid=(steps,),
+        in_specs=[
+            pl.BlockSpec((refs, total_rows), lambda j: (0, 0)),
+            pl.BlockSpec((total_rows, tile), lambda j: (0, j)),
+            pl.BlockSpec((total_rows, tile), lambda j: (0, j + steps)),
+            pl.BlockSpec((total_rows, LANES), lambda j: (0, width // LANES)),
+            pl.BlockSpec((refs, tile), lambda j: (0, j)),
+            pl.BlockSpec((refs, tile), lambda j: (0, j + steps)),
+        ],
+        out_specs=pl.BlockSpec((refs, 2, tile), lambda j: (0, 0, j)),
+        scratch_shapes=[pltpu.VMEM((refs, LANES), jnp.float32)],
+        compiler_params=pltpu.CompilerParams(vmem_limit_bytes=60 * 1024 * 1024),
+    )(weights, rows, rows, rows, temps, temps)
     evidence = evidence[:, :ND].reshape(ND, NX, NZ // ND, NY, ND, local)
     evidence = lax.dynamic_index_in_dim(evidence, lax.axis_index("dom"), 4, keepdims=False)
     evidence = jnp.transpose(evidence, (1, 3, 2, 0, 4)).reshape(-1)
-    return updated.reshape(refs, 2, quarter), evidence
+    return updated, evidence
 
 
 def solution(mesh):

time: 156 us -> 146 us (0.936)
  local copies, waits for them, and re-layouts: 14.5 us -> 1.26 us
  Pallas kernels: 131 us -> 141 us
  starting transfers between devices: 6.62 us -> 0 us
    pallas_call x0 -> x1, Pallas kernels: none -> 13.7 us  [on_device(): pl.pallas_call(update_kernel, out_shape=jax.ShapeDtypeStruct((refs, 2, qu...]
    all_to_all x1 -> x0, starting transfers between devices: 6.62 us -> none  [on_device(): lax.all_to_all(split, 'dom', split_axis=0, concat_axis=0, tiled=True)]
    reshape x1 -> x0, local copies, waits for them, and re-layouts: 6.57 us -> none  [on_device(): return (updated.reshape(refs, 2, quarter), evidence)]
    pallas_call x1, Pallas kernels: 131 us -> 127 us  [on_device(): pl.pallas_call(functools.partial(em_kernel, schedule, temp), out_shape=(j...]
    dynamic_slice x1 -> x0, local copies, waits for them, and re-layouts: 3.03 us -> none  [on_device(): lax.dynamic_slice_in_dim(templates, start, quarter, 2).reshape(refs, width)]
    unnamed x3 -> x2, local copies, waits for them, and re-layouts: 2.91 us -> 0.01 us
  transfers between devices with their start and end apart: 1 -> 0, of which waited for: 0 -> 0; matrix products, arithmetic and copies ran while one was open for 3% -> 0% of each run, Pallas kernels for 0% -> 0%
where the time goes in v2:
time: 146 us
  Pallas kernels  141 us (97%)
  other arithmetic  2.74 us (2%)
    pallas_call x1, Pallas kernels, on_device(): pl.pallas_call(functools.partial(em_kernel, schedule, temp), out_shape=(j...  127 us
    pallas_call x1, Pallas kernels, on_device(): pl.pallas_call(update_kernel, out_shape=jax.ShapeDtypeStruct((refs, 2, qu...  13.7 us

profile of v2, /device:TPU:1, one launch (start us, length us, event | category | flops | bytes accessed | tf_op | source)
XLA Modules:
  0.0 145.7 jit_solution(7817749546339881102)
XLA Ops:
  0.6 0.7 and_convert_fusion
  1.4 1.3 broadcast_multiply_fusion
  2.7 0.2 reshape.142
  2.8 0.2 copy.7
  3.0 0.7 pad_maximum_fusion.split
  3.7 127.2 %shard_map.59 = (bf16[2048,4224]{1,0:T(8,128)(2,1)}, bf16[256,4096]{1,0:T(8,128)(2,1)}, bf16[256,2048]{1,0:T(8,128)(2,1)}, f32[4,8,128]{2,1,0:T(8,128)}) custom-call(bf16[32,4224]{1,0:T(8,128)(2,1)} %pad_maximum_fusion.split, bf16[256,2,8192]{2,1,0:T(2,128)(2,1)} %templates.1), custom_call_target="tpu_custom_call" | custom-call | tf_op jit(solution)/shard_map/pallas_call | solution.py:405
  130.9 0.0 copy-start
  131.0 13.7 %shard_map.60 = f32[256,2,2048]{2,1,0:T(2,128)} custom-call(bf16[256,2048]{1,0:T(8,128)(2,1)} %get-tuple-element.6.weights, bf16[2048,4224]{1,0:T(8,128)(2,1)} %get-tuple-element.7.real.imag.mask, bf16[2048,4224]{1,0:T(8,128)(2,1)} %get-tuple-element.7.real.imag.mask, bf16[2048,4224]{1,0:T(8,128)(2,1)} %get-tuple-element.7.real.imag.mask, ...), custom_call_target="tpu_custom_call" | custom-call | tf_op jit(solution)/shard_map/pallas_call | solution.py:455
  144.7 0.0 copy-done
  144.7 0.2 reshape.143
  145.0 0.7 reshape.144
  (6 shorter events, 0.1 us)
Async XLA Ops:
  130.9 13.8 %copy-start = (f32[4,8,128]{2,1,0:T(8,128)S(1)}, f32[4,8,128]{2,1,0:T(8,128)}, u32[]{:S(2)}) copy-start(f32[4,8,128]{2,1,0:T(8,128)} %get-tuple-element.9) | copy-start | bytes 49156

commit v3 on v0

v3 whole, which is shorter than its diff:
```python
import functools
import math

import jax
import jax.numpy as jnp
from jax import lax
from jax.experimental import pallas as pl
from jax.experimental.pallas import tpu as pltpu
from jax.sharding import PartitionSpec as P

NBIN = 64
NX, NY, NZ, ND, NH = 2, 4, 8, 4, 2
LANES = 128
RING = (0, 7, 1, 6, 2, 5, 3, 4)
LINKS = ("x", "y+", "y-", "z+", "z-")
LATENCY = 3.0
TILE = 0.0879
BATCH = 128
UNIT = 16
LOW_AT, HIGH_AT = 19, 83
MESH = pl.DeviceIdType.MESH


def moved(unit, link):
    h, x, z, y = unit
    if link == "x":
        return h, 1 - x, z, y
    step = -1 if link[1] == "+" else 1
    return (h, x, (z + step) % NZ, y) if link[0] == "z" else (h, x, z, (y + step) % NY)

def plan(cols, first_a, second_a, x_cols, chain=(5.0, 6.0, 6.0, 6.0), compute=0.95):
    sends = []
    def add(link, unit, part, lo, hi, rank):
        sends.append(dict(link=link, unit=unit, part=part, lo=lo, hi=hi, rank=rank, lands=moved(unit, link)))
    for h in range(NH):
        add("x", (h, 0, 0, 0), "F", 0, cols, 0)
        for x in (0, 1):
            cut, end = (first_a, cols) if x == 0 else (second_a, cols - x_cols)
            plus = (x + h) % 2 == 0
            add("y+", (h, x, 0, 0), "A", 0, cut, 0)
            add("y-", (h, x, 0, 0), "A", 0, cut, 0)
            link, y = ("y+", 3) if plus else ("y-", 1)
            add(link, (h, x, 0, y), "A", 0, cut, 0)
            for k in range(4):
                if k < 3 or plus:
                    add("z+", (h, x, -k % NZ, 0), "B", cut, end, 1)
                if k < 3 or not plus:
                    add("z-", (h, x, k, 0), "B", cut, end, 1)
            for k in range(4):
                for y in (0, 3, 1, 2):
                    if k < 3 or y in (0, 3):
                        add("z+", (h, x, -k % NZ, y), "A", 0, cut, 2)
                    if k < 3 or y in (1, 2):
                        add("z-", (h, x, k, y), "A", 0, cut, 2)
            for n, z in enumerate(RING):
                add("y+", (h, x, z, 0), "B", cut, end, 2)
                add("y-", (h, x, z, 0), "B", cut, end, 2)
                link, y = ("y+", 3) if n % 2 == 0 else ("y-", 1)
                add(link, (h, x, z, y), "B", cut, end, 2)
            if x == 0 and x_cols:
                for z in RING:
                    for y in (0, 3, 1, 2):
                        if (z, y) != (0, 0):
                            add("x", (h, 0, z, y), "X", cols - x_cols, cols, 3)
    for number, s in enumerate(sends):
        s["id"] = number
    arrives = {(s["lands"], s["part"]): s["id"] for s in sends}
    for s in sends:
        h, x, z, y = s["unit"]
        if (x, z, y) == (0, 0, 0):
            s["needs"] = None
        elif (x, z, y) == (1, 0, 0):
            s["needs"] = arrives[s["unit"], "F"]
        else:
            s["needs"] = arrives[s["unit"], "B" if s["part"] == "X" else s["part"]]
    forwarded = {s["needs"] for s in sends}
    groups = {}
    for s in sends:
        key = (s["part"], s["lands"][:3]) if s["id"] not in forwarded else s["id"]
        groups.setdefault(key, []).append(s)
    for sem, members in enumerate(groups.values()):
        assert len({(s["lo"], s["hi"]) for s in members}) == 1
        for s in members:
            s["sem"], s["group"] = sem, len(members)
    free, landed, left = dict.fromkeys(LINKS, 0.0), {None: 0.0}, list(sends)
    when = {}; latest = dict.fromkeys(LINKS, 0.0)
    while left:
        best = None
        for s in left:
            if s["needs"] in landed:
                key = (max(landed[s["needs"]], free[s["link"]]), s["unit"][:2], s["rank"], s["id"])
                if best is None or key < best[0]:
                    best = key, s
        (start, *_), s = best
        free[s["link"]] = start + (s["hi"] - s["lo"]) * TILE
        landed[s["id"]] = free[s["link"]] + LATENCY
        latest[s["link"]] = max(latest[s["link"]], landed[s["needs"]])
        when[s["id"]] = latest[s["link"]]
        left.remove(s)
    events = [(when[s["id"]], 0, s["id"], s) for s in sends]
    batches = []
    for h in range(NH):
        for z in range(NZ):
            wanted = [arrives[(h, x, z, y), p] for x in range(NX) for y in range(NY) for p in "FABX" if ((h, x, z, y), p) in arrives]
            batches.append((max(landed[w] for w in wanted), h, z, wanted))
    batches.sort()
    return sends, events, batches, free


def timeline(schedule, lags):
    sends, events, batches, _ = schedule
    first = max(b[0] for b in batches if b[1] == 0)
    steps = [(first + sum(lags[: n + 1]), 2, n, None) for n in range(len(lags))]
    marked = [(b[0], 1, n, b) for n, b in enumerate(batches)]
    segments, issue, order = [], [], []
    for _, kind, n, what in sorted(events + marked + steps, key=lambda e: e[:3]):
        if kind == 1:
            segments.append((issue, what[3]))
            order.append((what[1], what[2]))
            issue = []
        else:
            issue.append(what if kind == 0 else n)
    assert not any(isinstance(e, dict) for e in issue)
    return segments, order, issue


def table(values, index):
    total = jnp.int32(0)
    for n, v in enumerate(values):
        if v:
            total = total + jnp.where(index == n, v, 0)
    return total


def em_kernel(
    sends, line, temp, whole_particles, bounds, templates,
    rows, temps, edge, num, weights_1, inverse, evid,
    particles, split, pairs, masks, weights_0, scores, parts, stat_a, stat_b, stat_z, stat_q, power,
    local_sem, load_sem, a_send, a_recv, send_sem, recv_sem,
    ps_send, ps_recv, z_send, z_recv, q_send, q_recv, w_send, w_recv, l_send, l_recv,
):
    segments, batches, late = line
    dom, orient = lax.axis_index("dom"), lax.axis_index("orient")
    x0, y0, z0 = orient // (NY * NZ), (orient // NZ) % NY, orient % NZ
    q0 = x0 * NY + y0
    refs, width = temps.shape
    quarter = width // 2
    half = rows.shape[0] // NH
    share = half // ND

    def at(x, y, z):
        return {"orient": (x * NY + y) * NZ + z}

    z_peer = [at(x0, y0, (z0 + k) % NZ) for k in range(NZ)]
    q_peer = [{"orient": (q0 + k) % (NX * NY) * NZ + z0} for k in range(NX * NY)]
    d_peer = [{"dom": (dom + k) % ND} for k in range(ND)]
    target = {
        "x": q_peer[NY],
        "y+": at(x0, (y0 + 1) % NY, z0),
        "y-": at(x0, (y0 + NY - 1) % NY, z0),
        "z+": z_peer[1],
        "z-": z_peer[NZ - 1],
    }
    chip_dom = dom + 1 - 2 * (dom % 2)
    side_dom = (dom + 2) % ND
    chip_peer, side_peer = {"dom": chip_dom}, {"dom": side_dom}

    load = pltpu.make_async_copy(
        templates.at[:, :, pl.ds(pl.multiple_of(dom * quarter, quarter), quarter)],
        pairs,
        load_sem,
    )
    fetch = pltpu.make_async_copy(whole_particles, particles, local_sem)
    fetch.start()
    load.start()
    barrier = pltpu.get_barrier_semaphore()
    greeted = list(target.values()) + d_peer[1:]
    for peer in greeted:
        pl.semaphore_signal(barrier, inc=1, device_id=peer, device_id_type=MESH)

    def remote(src, dst, ssem, rsem, peer):
        return pltpu.make_async_remote_copy(
            src_ref=src, dst_ref=dst, send_sem=ssem, recv_sem=rsem,
            device_id=peer, device_id_type=MESH,
        )

    z_at = [
        ((z0 + k) % NZ % ND * 2 + (z0 + k) % NZ // ND) * BATCH for k in range(NZ)
    ]
    y_at = [(y0 + k) % NY * UNIT for k in range(NY)]
    x_at = [x0 * NY * UNIT, (1 - x0) * NY * UNIT]

    def unit_row(unit):
        h, x, z, y = unit
        return h * half + x_at[x] + z_at[z] + y_at[y]

    def relayout(i, carry):
        r = pl.ds(pl.multiple_of(i * 16, 16), 16)
        for c in range(2):
            temps[r, c * quarter : (c + 1) * quarter] = pairs[r, c, :]
        return carry

    local = particles.shape[0]
    item = lax.broadcasted_iota(jnp.int32, (local, 1), 0)
    low, high = jnp.zeros((local, 1), jnp.float32), jnp.zeros((local, 1), jnp.float32)
    for n in range(local):
        low = jnp.where(item == n, bounds[0, n].astype(jnp.float32), low)
        high = jnp.where(item == n, bounds[1, n].astype(jnp.float32), high)
    column = lax.broadcasted_iota(jnp.int32, (local, quarter), 1)
    bins = (column * 37 % NBIN).astype(jnp.float32)
    seen = (low <= bins) & (bins < high)
    stash = jnp.where(column == LOW_AT, low, jnp.where(column == HIGH_AT, high, 0.0))
    fetch.wait()
    for c in range(2):
        for d in range(ND):
            piece = particles[:, c, d * quarter : (d + 1) * quarter].astype(jnp.float32)
            piece = jnp.where(seen, piece, stash if c == 0 else 0.0)
            split[d * local : (d + 1) * local, c * quarter : (c + 1) * quarter] = piece.astype(
                jnp.bfloat16
            )
    pl.semaphore_wait(barrier, len(greeted))

    own_at = unit_row((0, 0, 0, 0))

    def split_at(owner):
        return split.at[pl.ds(pl.multiple_of(owner * local, local), local)]

    def own_rows(source):
        row = own_at + source // 2 * half + source % 2 * local
        return rows.at[pl.ds(pl.multiple_of(row, local), local)]

    def a_copy(k, source, owner):
        return remote(split_at(owner), own_rows(source), a_send.at[k], a_recv.at[k], d_peer[k])

    for k in (2, 3, 1):
        a_copy(k, dom, (dom + k) % ND).start()
    own = pltpu.make_async_copy(split_at(dom), own_rows(dom), local_sem)
    own.start()
    own.wait()
    for k in (1, 2, 3):
        a_copy(k, (dom + ND - k) % ND, dom).wait_recv()
    def copy_of(s, unit):
        columns = pl.ds(s["lo"] * LANES, (s["hi"] - s["lo"]) * LANES)
        place = rows.at[pl.ds(pl.multiple_of(unit_row(unit), UNIT), UNIT), columns]
        return remote(
            place, place, send_sem.at[unit[0]], recv_sem.at[s["sem"]], target[s["link"]]
        )

    heard = set()

    def hear(number):
        if number is None or sends[number]["sem"] in heard:
            return
        s = sends[number]
        heard.add(s["sem"])
        h, x, z, _ = s["lands"]
        columns = pl.ds(s["lo"] * LANES, (s["hi"] - s["lo"]) * LANES)
        if s["group"] == 1:
            row = unit_row(s["lands"])
        else:
            row = h * half + x_at[x] + z_at[z]
        place = rows.at[pl.ds(pl.multiple_of(row, UNIT), UNIT * s["group"]), columns]
        remote(
            place, place, send_sem.at[h], recv_sem.at[s["sem"]], target[s["link"]]
        ).wait_recv()

    def partial_copy(slot):
        owner, part = slot % (2 * ND) // 2, slot // (2 * ND) * 2 + slot % 2
        rel = jnp.maximum((dom - owner + ND) % ND - 1, 0)
        return remote(
            scores.at[slot], parts.at[rel, part], ps_send.at[slot], ps_recv.at[rel, part],
            {"dom": owner},
        )

    def evidence_of(peak, mass):
        return jnp.concatenate([peak, mass, peak, mass], axis=0)

    def stat_copies(h, src, slots, index, peers, ssem, rsem):
        out = [
            remote(src.at[h], slots.at[h, index], ssem.at[h, k], rsem.at[h, k], peers[k])
            for k in range(1, len(peers))
        ]
        back = [
            remote(
                src.at[h], slots.at[h, (index + len(peers) - k) % len(peers)],
                ssem.at[h, k], rsem.at[h, k], peers[k],
            )
            for k in range(1, len(peers))
        ]
        return out, back

    def merged(h, slots):
        both = slots[h]
        peak = jnp.max(both[:, :2], axis=0)
        return peak, jnp.sum(both[:, 2:4] * jnp.exp(both[:, :2] - peak[None]), axis=0)

    z_stats = lambda h: stat_copies(h, stat_a, stat_z, z0, z_peer, z_send, z_recv)
    q_stats = lambda h: stat_copies(h, stat_b, stat_q, q0, q_peer, q_send, q_recv)

    def sum_scores(h):
        peaks, masses = [], []
        for k in range(2):
            part = h * 2 + k
            mine = h * 2 * ND + dom * 2 + k
            total = scores[mine]
            for rel in range(ND - 1):
                remote(
                    scores.at[mine], parts.at[rel, part], ps_send.at[mine],
                    ps_recv.at[rel, part], d_peer[1],
                ).wait_recv()
                total = total + parts[rel, part]
            total = total * temp
            parts[0, part] = total
            peak = jnp.max(total, axis=0, keepdims=True)
            peaks.append(peak)
            masses.append(jnp.sum(jnp.exp(total - peak), axis=0, keepdims=True))
        tile = evidence_of(jnp.concatenate(peaks, axis=0), jnp.concatenate(masses, axis=0))
        stat_a[h] = tile
        stat_z[h, z0] = tile
        for c in z_stats(h)[0]:
            c.start()

    def merge_z(h):
        for c in z_stats(h)[1]:
            c.wait_recv()
        tile = evidence_of(*merged(h, stat_z))
        stat_b[h] = tile
        stat_q[h, q0] = tile
        for c in q_stats(h)[0]:
            c.start()

    weights = (weights_0, weights_1)

    def w_copy(h, n, owner, peer):
        ref = weights[h].at[:, pl.ds(pl.multiple_of(owner * share, share), share)]
        return remote(ref, ref, w_send.at[h, n], w_recv.at[h, n], peer)

    def l_copy(h, k, owner):
        ref = evid.at[h, owner]
        return remote(ref, ref, l_send.at[h, k], l_recv.at[h, k], d_peer[k])

    def weigh(h):
        for c in q_stats(h)[1]:
            c.wait_recv()
        peak, mass = merged(h, stat_q)
        log_evidence = peak + jnp.log(mass)
        for k in range(2):
            w = jnp.exp(parts[0, h * 2 + k] - log_evidence[k : k + 1])
            place = pl.ds(pl.multiple_of(dom * share + k * BATCH, BATCH), BATCH)
            weights[h][:, place] = w.astype(jnp.bfloat16)
        evid[h, dom] = evidence_of(log_evidence, mass)
        w_copy(h, 0, dom, side_peer).start()
        w_copy(h, 1, dom, chip_peer).start()
        for k in range(1, ND):
            l_copy(h, k, dom).start()

    def forward(h):
        w_copy(h, 0, side_dom, side_peer).wait_recv()
        w_copy(h, 2, side_dom, chip_peer).start()

    def receive(h):
        w_copy(h, 1, chip_dom, chip_peer).wait_recv()
        w_copy(h, 2, (chip_dom + 2) % ND, chip_peer).wait_recv()

    def first_numerator(piece):
        def step(j, carry):
            columns = pl.ds(pl.multiple_of(piece * quarter + j * 256, 256), 256)
            num[:, columns] = jnp.dot(
                weights_0[...], rows[:half, columns], preferred_element_type=jnp.float32
            )
            return carry

        lax.fori_loop(0, quarter // 256, step, 0)

    chain = (sum_scores, merge_z, weigh, forward, receive)

    ready = []

    def prepare():
        load.wait()
        lax.fori_loop(0, refs // 16, relayout, 0)
        total = jnp.zeros((refs, LANES), jnp.float32)
        for c in range(width // LANES):
            piece = temps[:, c * LANES : (c + 1) * LANES].astype(jnp.float32)
            total = total + piece * piece
        total = 0.5 * total
        for c in range(3):
            head = total.astype(jnp.bfloat16)
            power[c] = head
            total = total - head.astype(jnp.float32)
        edge[...] = temps[:, :LANES]
        lane = lax.broadcasted_iota(jnp.int32, (refs, LANES), 1)
        stash = (lane == LOW_AT) | (lane == HIGH_AT)
        temps[:, :LANES] = jnp.where(
            stash, jnp.zeros((refs, LANES), jnp.bfloat16), temps[:, :LANES]
        )

    def phase_body(phase, carry):
        for n, (issue, wanted) in enumerate(segments):

            @pl.when(phase == n)
            def _(n=n, issue=issue, wanted=wanted):
                for s in issue:
                    if isinstance(s, int):
                        chain[s](0)
                    else:
                        if s["needs"] is not None and n == 0 and not ready:
                            prepare()
                            ready.append(True)
                        hear(s["needs"])
                        copy_of(s, s["unit"]).start()
                for w in wanted:
                    hear(w)

        bh = table([b[0] for b in batches], phase)
        bz = (z0 + table([b[1] for b in batches], phase)) % NZ
        place = bz % ND * 2 + bz // ND
        slot = bh * 2 * ND + place
        here = pl.ds(pl.multiple_of(slot * BATCH, BATCH), BATCH)
        bounds = rows[here, :LANES].astype(jnp.float32)
        lane = lax.broadcasted_iota(jnp.int32, (BATCH, LANES), 1)
        bins = (lane * 37 % NBIN).astype(jnp.float32)
        seen = (bins >= bounds[:, LOW_AT : LOW_AT + 1]) & (bins < bounds[:, HIGH_AT : HIGH_AT + 1])
        mask = jnp.where(seen, 1.0, 0.0).astype(jnp.bfloat16)
        masks[here, :] = mask
        nt = (((1,), (1,)), ((), ()))
        penalty = lax.dot_general(power[2], mask, nt, preferred_element_type=jnp.float32)
        for c in (1, 0):
            penalty = penalty + lax.dot_general(
                power[c], mask, nt, preferred_element_type=jnp.float32
            )
        corr = lax.dot_general(temps[...], rows[here, :], nt, preferred_element_type=jnp.float32)
        scores[slot] = corr - penalty

        @pl.when(place // 2 != dom)
        def _():
            partial_copy(slot).start()

        return carry

    lax.fori_loop(0, len(segments), phase_body, 0)

    for step in late:
        chain[step](0)
    sum_scores(1)
    first_numerator(0)
    merge_z(1)
    first_numerator(1)
    for h in range(NH):
        sent = sum((s["hi"] - s["lo"]) * UNIT for s in sends if s["unit"][0] == h)
        assert sent * LANES % width == 0 and sent * LANES // width <= half
        every = rows.at[pl.ds(0, sent * LANES // width)]
        pltpu.make_async_copy(every, every, send_sem.at[h]).wait()
    weigh(1)

    def drain(slot, carry):
        @pl.when(slot % (2 * ND) // 2 != dom)
        def _():
            partial_copy(slot).wait_send()

        return carry

    lax.fori_loop(0, NH * 2 * ND, drain, 0)
    for k in range(1, ND):
        a_copy(k, dom, (dom + k) % ND).wait_send()
    den = jnp.dot(weights_0[...], masks[:half], preferred_element_type=jnp.float32)
    inverse[...] = den
    forward(1)
    for h in range(NH):
        for c in z_stats(h)[0] + q_stats(h)[0]:
            c.wait_send()
    receive(1)
    den = inverse[...] + jnp.dot(weights_1[...], masks[half:], preferred_element_type=jnp.float32)
    inverse[...] = 1.0 / (den + 1.0)
    for h in range(NH):
        for k in range(1, ND):
            l_copy(h, k, (dom + ND - k) % ND).wait_recv()
    for h in range(NH):
        for k in range(1, ND):
            l_copy(h, k, dom).wait_send()
        w_copy(h, 0, dom, side_peer).wait_send()
        w_copy(h, 1, dom, chip_peer).wait_send()
        w_copy(h, 2, side_dom, chip_peer).wait_send()


def update_kernel(weights, inverse, rows, num, temps, edge, evid, out, evid_out, staged, sems):
    refs, width = num.shape
    quarter, half = width // 2, weights.shape[1]
    tile = staged.shape[3]
    evid_out[...] = evid[...]

    def copy(j):
        columns = pl.ds(pl.multiple_of(j * tile, tile), tile)
        return pltpu.make_async_copy(staged.at[j % 2], out.at[:, :, columns], sems.at[j % 2])

    lane = lax.broadcasted_iota(jnp.int32, (refs, LANES), 1)
    stash = (lane == LOW_AT) | (lane == HIGH_AT)
    scale = jnp.concatenate([inverse[...]] * (tile // LANES), axis=1)

    def step(j, carry):
        @pl.when(j >= 2)
        def _():
            copy(j - 2).wait()

        for c in range(2):
            columns = pl.ds(pl.multiple_of(c * quarter + j * tile, tile), tile)
            total = num[:, columns] + jnp.dot(
                weights[...], rows[half:, columns], preferred_element_type=jnp.float32
            )
            staged[j % 2, :, c, :] = (total + temps[:, columns].astype(jnp.float32)) * scale

        @pl.when(j == 0)
        def _():
            first = staged[0, :, 0, :LANES]
            kept = edge[...].astype(jnp.float32) * inverse[...]
            staged[0, :, 0, :LANES] = jnp.where(stash, kept, first)

        copy(j).start()
        return carry

    steps = quarter // tile
    lax.fori_loop(0, steps, step, 0)
    copy(steps - 2).wait()
    copy(steps - 1).wait()


def on_device(particles, templates, tilt_low, tilt_high):
    local, _, band = particles.shape
    refs = templates.shape[0]
    quarter = band // ND
    width = 2 * quarter
    temp = 3.0 / math.sqrt(band)
    bounds = jnp.stack([tilt_low, tilt_high])

    schedule = plan(width // LANES, 13, 7, 10)
    line = timeline(schedule, (9.0, 6.0, 9.0, 8.0, 4.0))
    count = 1 + max(s["sem"] for s in schedule[0])
    total = NX * NY * NZ * ND * local
    half = total // NH
    bf16, f32 = jnp.bfloat16, jnp.float32
    dma = pltpu.SemaphoreType.DMA
    vmem = pl.BlockSpec(memory_space=pltpu.VMEM)
    rows, temps, edge, num, weights, inverse, evidence = pl.pallas_call(
        functools.partial(em_kernel, schedule[0], line, temp),
        out_shape=(
            jax.ShapeDtypeStruct((total, width), bf16),
            jax.ShapeDtypeStruct((refs, width), bf16),
            jax.ShapeDtypeStruct((refs, LANES), bf16),
            jax.ShapeDtypeStruct((refs, width), f32),
            jax.ShapeDtypeStruct((refs, half), bf16),
            jax.ShapeDtypeStruct((refs, LANES), f32),
            jax.ShapeDtypeStruct((NH, ND, 8, LANES), f32),
        ),
        in_specs=[
            pl.BlockSpec(memory_space=pltpu.HBM),
            pl.BlockSpec(memory_space=pltpu.SMEM),
            pl.BlockSpec(memory_space=pltpu.HBM),
        ],
        out_specs=(vmem,) * 7,
        scratch_shapes=[
            pltpu.VMEM(particles.shape, bf16),
            pltpu.VMEM((ND * local, width), bf16),
            pltpu.VMEM((refs, 2, quarter), bf16),
            pltpu.VMEM((total, LANES), bf16),
            pltpu.VMEM((refs, half), bf16),
            pltpu.VMEM((NH * 2 * ND, refs, LANES), f32),
            pltpu.VMEM((ND - 1, NH * 2, refs, LANES), f32),
            pltpu.VMEM((NH, 8, LANES), f32),
            pltpu.VMEM((NH, 8, LANES), f32),
            pltpu.VMEM((NH, NZ, 8, LANES), f32),
            pltpu.VMEM((NH, NX * NY, 8, LANES), f32),
            pltpu.VMEM((3, refs, LANES), bf16),
            dma(()),
            dma(()),
            dma((ND,)),
            dma((ND,)),
            dma((NH,)),
            dma((count,)),
            dma((NH * 2 * ND,)),
            dma((ND - 1, NH * 2)),
            dma((NH, NZ)),
            dma((NH, NZ)),
            dma((NH, NX * NY)),
            dma((NH, NX * NY)),
            dma((NH, 3)),
            dma((NH, 3)),
            dma((NH, ND)),
            dma((NH, ND)),
        ],
        compiler_params=pltpu.CompilerParams(
            collective_id=0, has_side_effects=True, vmem_limit_bytes=12 * 1024 * 1024
        ),
    )(
        pltpu.with_memory_space_constraint(particles, pltpu.HBM),
        bounds,
        pltpu.with_memory_space_constraint(templates, pltpu.HBM),
    )
    tile = 256
    updated, evidence = pl.pallas_call(
        update_kernel,
        out_shape=(
            jax.ShapeDtypeStruct((refs, 2, quarter), f32),
            jax.ShapeDtypeStruct(evidence.shape, f32),
        ),
        in_specs=[vmem] * 7,
        out_specs=(pl.BlockSpec(memory_space=pltpu.HBM), vmem),
        scratch_shapes=[pltpu.VMEM((2, refs, 2, tile), f32), dma((2,))],
        compiler_params=pltpu.CompilerParams(vmem_limit_bytes=8 * 1024 * 1024),
    )(weights, inverse, rows, num, temps, edge, evidence)
    evidence = evidence[:, :, :2].reshape(NH, ND, 2, NX, NY, 2, local)
    dom = lax.axis_index("dom")
    evidence = lax.dynamic_index_in_dim(evidence, dom // 2, 0, keepdims=False)
    evidence = lax.dynamic_index_in_dim(evidence, dom % 2, 4, keepdims=False)
    evidence = jnp.transpose(evidence, (2, 3, 1, 0, 4)).reshape(-1)
    return updated, evidence


def solution(mesh):
    in_specs = (
        P(("dom", "orient"), None, None),
        P("orient", None, None),
        P(("dom", "orient")),
        P(("dom", "orient")),
    )
    out_specs = (P("orient", None, "dom"), P("dom"))
    return jax.shard_map(
        on_device, mesh=mesh, in_specs=in_specs, out_specs=out_specs, check_vma=False
    )
```

time: 445 us -> 130 us (0.29)
  waiting for transfers between devices: 205 us -> 0 us
  Pallas kernels: 0 us -> 128 us
  local copies, waits for them, and re-layouts: 126 us -> 0.97 us
  other arithmetic: 46 us -> 0.68 us
  matrix products: 39 us -> 0 us
  between operations: 14.2 us -> 0.71 us
  starting transfers between devices: 12.6 us -> 0 us
    all_gather x1 -> x0, waiting for transfers between devices: 142 us -> none  [side_by_side(): filled = lax.all_gather(both, axis, axis=dim, tiled=True)]
    pallas_call x0 -> x2, Pallas kernels: none -> 128 us  [the longest x1 121 us: on_device(): pl.pallas_call(functools.partial(em_kernel, schedule[0], line, temp), out...]
    unnamed x9 -> x0, local copies, waits for them, and re-layouts: 70.8 us -> none
    reduce_scatter x1 -> x0, waiting for transfers between devices: 62.6 us -> none  [on_device(): lax.psum_scatter(numerator.astype(jnp.bfloat16), 'dom', scatter_dimension...]
    dot_general x4 -> x0, matrix products: 39 us -> none  [the longest x1 26.5 us: on_device(): lax.dot_general(flat_rows, template_flat, (((1,), (1,)), ((), ())), prefe...]
    slice x22 -> x1, local copies, waits for them, and re-layouts: 27.3 us -> 0.01 us  [on_device(): evidence = evidence[:, :, :2].reshape(NH, ND, 2, NX, NY, 2, local)]
    mul x1 -> x0, other arithmetic: 22.4 us -> none  [on_device(): masked = gathered * observed[:, None, :]]
    dot_general x1 -> x0, local copies, waits for them, and re-layouts: 22.4 us -> none  [on_device(): lax.dot_general(weights, flat_rows, (((0,), (0,)), ((), ())), preferred_e...]
  transfers between devices with their start and end apart: 4 -> 0, of which waited for: 2 -> 0; matrix products, arithmetic and copies ran while one was open for 30% -> 0% of each run, Pallas kernels for 0% -> 0%
where the time goes in v3:
time: 130 us
  Pallas kernels  128 us (98%)
    pallas_call x1, Pallas kernels, on_device(): pl.pallas_call(functools.partial(em_kernel, schedule[0], line, temp), out...  121 us
    pallas_call x1, Pallas kernels, on_device(): pl.pallas_call(update_kernel, out_shape=(jax.ShapeDtypeStruct((refs, 2, q...  6.6 us

profile of v3, /device:TPU:1, one launch (start us, length us, event | category | flops | bytes accessed | tf_op | source)
XLA Modules:
  0.0 130.1 jit_solution(15768842788257297236)
XLA Ops:
  0.6 0.7 pad_add_fusion.bounds
  1.3 121.2 %shard_map.59 = (bf16[2048,4096]{1,0:T(8,128)(2,1)S(1)}, bf16[256,4096]{1,0:T(8,128)(2,1)S(1)}, bf16[256,128]{1,0:T(8,128)(2,1)S(1)}, f32[256,4096]{1,0:T(8,128)...) custom-call(bf16[8,2,8192]{2,1,0:T(2,128)(2,1)} %whole_particles.1, ...), custom_call_target="tpu_custom_call" | custom-call | tf_op jit(solution)/shard_map/pallas_call | solution.py:543
  122.5 6.6 %shard_map.60 = (f32[256,2,2048]{2,1,0:T(2,128)}, f32[2,4,8,128]{3,2,1,0:T(8,128)S(1)}) custom-call(bf16[256,1024]{1,0:T(8,128)(2,1)S(1)} %get-tuple-element.11.weights, f32[256,128]{1,0:T(8,128)S(1)} %get-tuple-element.12.inverse, bf16[2048,4096]{1,0:T(8,128)(2,1)S(1)} %get-tuple-element.13.rows, f32[256,4096]{1,0:T(8,128)S(1)} %get-tuple-element.14.num, ...), custom_call_target="tpu_custom_call" | custom-call | tf_op jit(solution)/shard_map/pallas_call | solution.py:599
  129.1 0.2 reshape.12
  129.5 0.7 reshape.13
  (3 shorter events, 0.1 us)

commit v4 on v3

--- a/solution.py
+++ b/solution.py
@@ -13,8 +13,13 @@
 LANES = 128
 RING = (0, 7, 1, 6, 2, 5, 3, 4)
 LINKS = ("x", "y+", "y-", "z+", "z-")
-LATENCY = 3.0
+LATENCY = 3.75
 TILE = 0.0879
+AHEAD = 2.0
+CUTS = ((13, 8, 14), (13, 8, 9))
+RANKS = (3, 2, 2, 3, 0)
+LAGS = (2.5, 11.0, 9.0)
+PREPARE_AT, PREPARE_STEP, PREPARE_PARTS = 6.0, 3.0, 8
 BATCH = 128
 UNIT = 16
 LOW_AT, HIGH_AT = 19, 83
@@ -28,40 +33,41 @@
     step = -1 if link[1] == "+" else 1
     return (h, x, (z + step) % NZ, y) if link[0] == "z" else (h, x, z, (y + step) % NY)
 
-def plan(cols, first_a, second_a, x_cols, chain=(5.0, 6.0, 6.0, 6.0), compute=0.95):
+def plan(cols, cuts, ranks=(0, 1, 2, 2, 3)):
     sends = []
     def add(link, unit, part, lo, hi, rank):
         sends.append(dict(link=link, unit=unit, part=part, lo=lo, hi=hi, rank=rank, lands=moved(unit, link)))
     for h in range(NH):
+        first_a, second_a, x_cols = cuts[h]
         add("x", (h, 0, 0, 0), "F", 0, cols, 0)
         for x in (0, 1):
             cut, end = (first_a, cols) if x == 0 else (second_a, cols - x_cols)
             plus = (x + h) % 2 == 0
-            add("y+", (h, x, 0, 0), "A", 0, cut, 0)
-            add("y-", (h, x, 0, 0), "A", 0, cut, 0)
+            add("y+", (h, x, 0, 0), "A", 0, cut, ranks[0])
+            add("y-", (h, x, 0, 0), "A", 0, cut, ranks[0])
             link, y = ("y+", 3) if plus else ("y-", 1)
-            add(link, (h, x, 0, y), "A", 0, cut, 0)
+            add(link, (h, x, 0, y), "A", 0, cut, ranks[0])
             for k in range(4):
                 if k < 3 or plus:
-                    add("z+", (h, x, -k % NZ, 0), "B", cut, end, 1)
+                    add("z+", (h, x, -k % NZ, 0), "B", cut, end, ranks[1])
                 if k < 3 or not plus:
-                    add("z-", (h, x, k, 0), "B", cut, end, 1)
+                    add("z-", (h, x, k, 0), "B", cut, end, ranks[1])
             for k in range(4):
                 for y in (0, 3, 1, 2):
                     if k < 3 or y in (0, 3):
-                        add("z+", (h, x, -k % NZ, y), "A", 0, cut, 2)
+                        add("z+", (h, x, -k % NZ, y), "A", 0, cut, ranks[2])
                     if k < 3 or y in (1, 2):
-                        add("z-", (h, x, k, y), "A", 0, cut, 2)
+                        add("z-", (h, x, k, y), "A", 0, cut, ranks[2])
             for n, z in enumerate(RING):
-                add("y+", (h, x, z, 0), "B", cut, end, 2)
-                add("y-", (h, x, z, 0), "B", cut, end, 2)
+                add("y+", (h, x, z, 0), "B", cut, end, ranks[3])
+                add("y-", (h, x, z, 0), "B", cut, end, ranks[3])
                 link, y = ("y+", 3) if n % 2 == 0 else ("y-", 1)
-                add(link, (h, x, z, y), "B", cut, end, 2)
+                add(link, (h, x, z, y), "B", cut, end, ranks[3])
             if x == 0 and x_cols:
                 for z in RING:
                     for y in (0, 3, 1, 2):
                         if (z, y) != (0, 0):
-                            add("x", (h, 0, z, y), "X", cols - x_cols, cols, 3)
+                            add("x", (h, 0, z, y), "X", cols - x_cols, cols, ranks[4])
     for number, s in enumerate(sends):
         s["id"] = number
     arrives = {(s["lands"], s["part"]): s["id"] for s in sends}
@@ -94,7 +100,8 @@
         (start, *_), s = best
         free[s["link"]] = start + (s["hi"] - s["lo"]) * TILE
         landed[s["id"]] = free[s["link"]] + LATENCY
-        latest[s["link"]] = max(latest[s["link"]], landed[s["needs"]])
+        early = start - AHEAD if s["part"] == "X" else 0.0
+        latest[s["link"]] = max(latest[s["link"]], landed[s["needs"]], early)
         when[s["id"]] = latest[s["link"]]
         left.remove(s)
     events = [(when[s["id"]], 0, s["id"], s) for s in sends]
@@ -109,9 +116,15 @@
 
 def timeline(schedule, lags):
     sends, events, batches, _ = schedule
-    first = max(b[0] for b in batches if b[1] == 0)
+    couples = [
+        (two[1][0], two[0][1], (two[0][2], two[1][2]), two[0][3] + two[1][3])
+        for two in zip(batches[::2], batches[1::2])
+    ]
+    assert all(one[1] == other[1] for one, other in zip(batches[::2], batches[1::2]))
+    first = max(b[0] for b in couples if b[1] == 0)
     steps = [(first + sum(lags[: n + 1]), 2, n, None) for n in range(len(lags))]
-    marked = [(b[0], 1, n, b) for n, b in enumerate(batches)]
+    marked = [(b[0], 1, n, b) for n, b in enumerate(couples)]
+    marked += [(PREPARE_AT + n * PREPARE_STEP, 3, n, None) for n in range(PREPARE_PARTS)]
     segments, issue, order = [], [], []
     for _, kind, n, what in sorted(events + marked + steps, key=lambda e: e[:3]):
         if kind == 1:
@@ -119,9 +132,14 @@
             order.append((what[1], what[2]))
             issue = []
         else:
-            issue.append(what if kind == 0 else n)
+            issue.append(what if kind == 0 else (kind, n))
     assert not any(isinstance(e, dict) for e in issue)
     return segments, order, issue
+
+
+def same(one, other):
+    keys = ("link", "part", "lo", "hi")
+    return all(one[k] == other[k] for k in keys)
 
 
 def table(values, index):
@@ -135,9 +153,9 @@
 def em_kernel(
     sends, line, temp, whole_particles, bounds, templates,
     rows, temps, edge, num, weights_1, inverse, evid,
-    particles, split, pairs, masks, weights_0, scores, parts, stat_a, stat_b, stat_z, stat_q, power,
+    particles, split, pairs, masks, weights_0, scores, core_parts, parts, totals, stat_a, stat_b, stat_z, stat_q, power,
     local_sem, load_sem, a_send, a_recv, send_sem, recv_sem,
-    ps_send, ps_recv, z_send, z_recv, q_send, q_recv, w_send, w_recv, l_send, l_recv,
+    ps_send, pc_recv, px_recv, z_send, z_recv, q_send, q_recv, t_send, t_recv, l_send, l_recv,
 ):
     segments, batches, late = line
     dom, orient = lax.axis_index("dom"), lax.axis_index("orient")
@@ -229,16 +247,17 @@
         row = own_at + source // 2 * half + source % 2 * local
         return rows.at[pl.ds(pl.multiple_of(row, local), local)]
 
+    diag_dom = (chip_dom + 2) % ND
+    others = ((chip_dom, chip_peer), (side_dom, side_peer), (diag_dom, {"dom": diag_dom}))
+
     def a_copy(k, source, owner):
-        return remote(split_at(owner), own_rows(source), a_send.at[k], a_recv.at[k], d_peer[k])
-
-    for k in (2, 3, 1):
-        a_copy(k, dom, (dom + k) % ND).start()
+        return remote(split_at(owner), own_rows(source), a_send.at[k], a_recv.at[k], others[k][1])
+
+    for k in (1, 2, 0):
+        a_copy(k, dom, others[k][0]).start()
     own = pltpu.make_async_copy(split_at(dom), own_rows(dom), local_sem)
     own.start()
-    own.wait()
-    for k in (1, 2, 3):
-        a_copy(k, (dom + ND - k) % ND, dom).wait_recv()
+
     def copy_of(s, unit):
         columns = pl.ds(s["lo"] * LANES, (s["hi"] - s["lo"]) * LANES)
         place = rows.at[pl.ds(pl.multiple_of(unit_row(unit), UNIT), UNIT), columns]
@@ -264,13 +283,29 @@
             place, place, send_sem.at[h], recv_sem.at[s["sem"]], target[s["link"]]
         ).wait_recv()
 
-    def partial_copy(slot):
-        owner, part = slot % (2 * ND) // 2, slot // (2 * ND) * 2 + slot % 2
-        rel = jnp.maximum((dom - owner + ND) % ND - 1, 0)
+    def owner_of(slot):
+        return slot % (2 * ND) // 2
+
+    def core_copy(slot):
         return remote(
-            scores.at[slot], parts.at[rel, part], ps_send.at[slot], ps_recv.at[rel, part],
-            {"dom": owner},
+            scores.at[slot], core_parts.at[slot], ps_send.at[slot], pc_recv.at[slot], chip_peer
         )
+
+    def side_copy(slot):
+        part = slot // (2 * ND) * 2 + slot % 2
+        return remote(
+            scores.at[slot], parts.at[part], ps_send.at[slot], px_recv.at[part], side_peer
+        )
+
+    def combine(slot):
+        @pl.when(owner_of(slot) % 2 == dom % 2)
+        def _():
+            core_copy(slot).wait_recv()
+            scores[slot] = scores[slot] + core_parts[slot]
+
+            @pl.when(owner_of(slot) != dom)
+            def _():
+                side_copy(slot).start()
 
     def evidence_of(peak, mass):
         return jnp.concatenate([peak, mass, peak, mass], axis=0)
@@ -297,20 +332,17 @@
     z_stats = lambda h: stat_copies(h, stat_a, stat_z, z0, z_peer, z_send, z_recv)
     q_stats = lambda h: stat_copies(h, stat_b, stat_q, q0, q_peer, q_send, q_recv)
 
+    def total_copy(h, n, k, owner, peer):
+        ref = totals.at[h, owner, k]
+        return remote(ref, ref, t_send.at[h, n, k], t_recv.at[h, n, k], peer)
+
     def sum_scores(h):
         peaks, masses = [], []
         for k in range(2):
-            part = h * 2 + k
             mine = h * 2 * ND + dom * 2 + k
-            total = scores[mine]
-            for rel in range(ND - 1):
-                remote(
-                    scores.at[mine], parts.at[rel, part], ps_send.at[mine],
-                    ps_recv.at[rel, part], d_peer[1],
-                ).wait_recv()
-                total = total + parts[rel, part]
-            total = total * temp
-            parts[0, part] = total
+            side_copy(mine).wait_recv()
+            total = (scores[mine] + parts[h * 2 + k]) * temp
+            totals[h, dom, k] = total
             peak = jnp.max(total, axis=0, keepdims=True)
             peaks.append(peak)
             masses.append(jnp.sum(jnp.exp(total - peak), axis=0, keepdims=True))
@@ -319,6 +351,9 @@
         stat_z[h, z0] = tile
         for c in z_stats(h)[0]:
             c.start()
+        total_copy(h, 0, 0, dom, side_peer).start()
+        for k in range(2):
+            total_copy(h, 1, k, dom, chip_peer).start()
 
     def merge_z(h):
         for c in z_stats(h)[1]:
@@ -328,12 +363,9 @@
         stat_q[h, q0] = tile
         for c in q_stats(h)[0]:
             c.start()
+        total_copy(h, 0, 1, dom, side_peer).start()
 
     weights = (weights_0, weights_1)
-
-    def w_copy(h, n, owner, peer):
-        ref = weights[h].at[:, pl.ds(pl.multiple_of(owner * share, share), share)]
-        return remote(ref, ref, w_send.at[h, n], w_recv.at[h, n], peer)
 
     def l_copy(h, k, owner):
         ref = evid.at[h, owner]
@@ -344,41 +376,55 @@
             c.wait_recv()
         peak, mass = merged(h, stat_q)
         log_evidence = peak + jnp.log(mass)
-        for k in range(2):
-            w = jnp.exp(parts[0, h * 2 + k] - log_evidence[k : k + 1])
-            place = pl.ds(pl.multiple_of(dom * share + k * BATCH, BATCH), BATCH)
-            weights[h][:, place] = w.astype(jnp.bfloat16)
         evid[h, dom] = evidence_of(log_evidence, mass)
-        w_copy(h, 0, dom, side_peer).start()
-        w_copy(h, 1, dom, chip_peer).start()
         for k in range(1, ND):
             l_copy(h, k, dom).start()
+        fill_weights(h, dom, log_evidence)
+
+    def fill_weights(h, owner, log_evidence):
+        for k in range(2):
+            w = jnp.exp(totals[h, owner, k] - log_evidence[k : k + 1])
+            place = pl.ds(pl.multiple_of(owner * share + k * BATCH, BATCH), BATCH)
+            weights[h][:, place] = w.astype(jnp.bfloat16)
 
     def forward(h):
-        w_copy(h, 0, side_dom, side_peer).wait_recv()
-        w_copy(h, 2, side_dom, chip_peer).start()
+        for k in range(2):
+            total_copy(h, 0, k, side_dom, side_peer).wait_recv()
+            total_copy(h, 2, k, side_dom, chip_peer).start()
 
     def receive(h):
-        w_copy(h, 1, chip_dom, chip_peer).wait_recv()
-        w_copy(h, 2, (chip_dom + 2) % ND, chip_peer).wait_recv()
+        for k in range(2):
+            total_copy(h, 1, k, chip_dom, chip_peer).wait_recv()
+            total_copy(h, 2, k, diag_dom, chip_peer).wait_recv()
+
+    def fill_others(h):
+        for k in range(1, ND):
+            owner = (dom + ND - k) % ND
+            l_copy(h, k, owner).wait_recv()
+            fill_weights(h, owner, evid[h, owner][:2])
 
     def first_numerator(piece):
-        def step(j, carry):
-            columns = pl.ds(pl.multiple_of(piece * quarter + j * 256, 256), 256)
-            num[:, columns] = jnp.dot(
-                weights_0[...], rows[:half, columns], preferred_element_type=jnp.float32
-            )
-            return carry
-
-        lax.fori_loop(0, quarter // 256, step, 0)
-
-    chain = (sum_scores, merge_z, weigh, forward, receive)
-
-    ready = []
-
-    def prepare():
-        load.wait()
-        lax.fori_loop(0, refs // 16, relayout, 0)
+        columns = pl.ds(piece * quarter, quarter)
+        num[:, columns] = jnp.dot(
+            weights_0[...], rows[:half, columns], preferred_element_type=jnp.float32
+        )
+
+    last_of = [max(n for n, b in enumerate(batches) if b[0] == h) for h in range(NH)]
+    assert last_of == [len(batches) // 2 - 1, len(batches) - 1]
+
+    def combine_last(h):
+        for slot in slots_of(last_of[h]):
+            combine(slot)
+
+    chain = (combine_last, sum_scores, merge_z)
+
+    def prepare(part):
+        if part == 0:
+            load.wait()
+        share_of = refs // 16 // PREPARE_PARTS
+        lax.fori_loop(part * share_of, (part + 1) * share_of, relayout, 0)
+        if part < PREPARE_PARTS - 1:
+            return
         total = jnp.zeros((refs, LANES), jnp.float32)
         for c in range(width // LANES):
             piece = temps[:, c * LANES : (c + 1) * LANES].astype(jnp.float32)
@@ -395,92 +441,134 @@
             stash, jnp.zeros((refs, LANES), jnp.bfloat16), temps[:, :LANES]
         )
 
+    def slots_of(phase):
+        bh = table([b[0] for b in batches], phase)
+        slots = []
+        for n in range(2):
+            bz = (z0 + table([b[1][n] for b in batches], phase)) % NZ
+            slots.append(bh * 2 * ND + bz % ND * 2 + bz // ND)
+        return slots
+
+    opening = [s for s in sends if s["needs"] is None]
+    twins = [(s, next(t for t in opening if t["unit"][0] == 1 and same(s, t)))
+             for s in opening if s["unit"][0] == 0]
+    near = dom // 2
+    own.wait()
+    a_copy(0, chip_dom, dom).wait_recv()
+    for h in (near, 1 - near):
+        for s, t in twins:
+            columns = pl.ds(s["lo"] * LANES, (s["hi"] - s["lo"]) * LANES)
+            row = unit_row((h, 0, 0, 0))
+            place = rows.at[pl.ds(pl.multiple_of(row, UNIT), UNIT), columns]
+            sem = s["sem"] + h * (t["sem"] - s["sem"])
+            remote(
+                place, place, send_sem.at[h], recv_sem.at[sem], target[s["link"]]
+            ).start()
+        if h is near:
+            for k in (1, 2):
+                a_copy(k, others[k][0], dom).wait_recv()
+
     def phase_body(phase, carry):
         for n, (issue, wanted) in enumerate(segments):
 
             @pl.when(phase == n)
             def _(n=n, issue=issue, wanted=wanted):
                 for s in issue:
-                    if isinstance(s, int):
-                        chain[s](0)
+                    if isinstance(s, dict) and s["needs"] is None:
+                        continue
+                    if isinstance(s, tuple):
+                        if s[0] == 3:
+                            prepare(s[1])
+                        else:
+                            chain[s[1]](0)
                     else:
-                        if s["needs"] is not None and n == 0 and not ready:
-                            prepare()
-                            ready.append(True)
                         hear(s["needs"])
                         copy_of(s, s["unit"]).start()
                 for w in wanted:
                     hear(w)
 
-        bh = table([b[0] for b in batches], phase)
-        bz = (z0 + table([b[1] for b in batches], phase)) % NZ
-        place = bz % ND * 2 + bz // ND
-        slot = bh * 2 * ND + place
-        here = pl.ds(pl.multiple_of(slot * BATCH, BATCH), BATCH)
-        bounds = rows[here, :LANES].astype(jnp.float32)
+        slots = slots_of(phase)
+        heres = [pl.ds(pl.multiple_of(slot * BATCH, BATCH), BATCH) for slot in slots]
         lane = lax.broadcasted_iota(jnp.int32, (BATCH, LANES), 1)
         bins = (lane * 37 % NBIN).astype(jnp.float32)
-        seen = (bins >= bounds[:, LOW_AT : LOW_AT + 1]) & (bins < bounds[:, HIGH_AT : HIGH_AT + 1])
-        mask = jnp.where(seen, 1.0, 0.0).astype(jnp.bfloat16)
-        masks[here, :] = mask
+        both = []
+        for here in heres:
+            lims = rows[here, :LANES].astype(jnp.float32)
+            seen = (bins >= lims[:, LOW_AT : LOW_AT + 1]) & (bins < lims[:, HIGH_AT : HIGH_AT + 1])
+            mask = jnp.where(seen, 1.0, 0.0).astype(jnp.bfloat16)
+            masks[here, :] = mask
+            both.append(mask)
+        mask = jnp.concatenate(both, axis=0)
         nt = (((1,), (1,)), ((), ()))
         penalty = lax.dot_general(power[2], mask, nt, preferred_element_type=jnp.float32)
         for c in (1, 0):
             penalty = penalty + lax.dot_general(
                 power[c], mask, nt, preferred_element_type=jnp.float32
             )
-        corr = lax.dot_general(temps[...], rows[here, :], nt, preferred_element_type=jnp.float32)
-        scores[slot] = corr - penalty
-
-        @pl.when(place // 2 != dom)
+        batch = jnp.concatenate([rows[here, :] for here in heres], axis=0)
+        corr = lax.dot_general(temps[...], batch, nt, preferred_element_type=jnp.float32)
+        result = corr - penalty
+        for n, slot in enumerate(slots):
+            scores[slot] = result[:, n * BATCH : (n + 1) * BATCH]
+
+            @pl.when(owner_of(slot) % 2 != dom % 2)
+            def _(slot=slot):
+                core_copy(slot).start()
+
+        @pl.when((phase > 0) & (phase != last_of[0] + 1))
         def _():
-            partial_copy(slot).start()
+            for slot in slots_of(phase - 1):
+                combine(slot)
 
         return carry
 
     lax.fori_loop(0, len(segments), phase_body, 0)
 
     for step in late:
-        chain[step](0)
+        chain[step[1]](0)
+    combine_last(1)
+    forward(0)
     sum_scores(1)
+    weigh(0)
+    receive(0)
+    merge_z(1)
+    fill_others(0)
     first_numerator(0)
-    merge_z(1)
-    first_numerator(1)
+    forward(1)
     for h in range(NH):
         sent = sum((s["hi"] - s["lo"]) * UNIT for s in sends if s["unit"][0] == h)
         assert sent * LANES % width == 0 and sent * LANES // width <= half
         every = rows.at[pl.ds(0, sent * LANES // width)]
         pltpu.make_async_copy(every, every, send_sem.at[h]).wait()
+    first_numerator(1)
+    receive(1)
     weigh(1)
 
     def drain(slot, carry):
-        @pl.when(slot % (2 * ND) // 2 != dom)
+        @pl.when(owner_of(slot) != dom)
         def _():
-            partial_copy(slot).wait_send()
+            core_copy(slot).wait_send()
 
         return carry
 
     lax.fori_loop(0, NH * 2 * ND, drain, 0)
-    for k in range(1, ND):
-        a_copy(k, dom, (dom + k) % ND).wait_send()
-    den = jnp.dot(weights_0[...], masks[:half], preferred_element_type=jnp.float32)
-    inverse[...] = den
-    forward(1)
+    for k in range(ND - 1):
+        a_copy(k, dom, others[k][0]).wait_send()
     for h in range(NH):
         for c in z_stats(h)[0] + q_stats(h)[0]:
             c.wait_send()
-    receive(1)
+        for k in range(2):
+            total_copy(h, 0, k, dom, side_peer).wait_send()
+            total_copy(h, 1, k, dom, chip_peer).wait_send()
+            total_copy(h, 2, k, side_dom, chip_peer).wait_send()
+    den = jnp.dot(weights_0[...], masks[:half], preferred_element_type=jnp.float32)
+    inverse[...] = den
+    fill_others(1)
     den = inverse[...] + jnp.dot(weights_1[...], masks[half:], preferred_element_type=jnp.float32)
     inverse[...] = 1.0 / (den + 1.0)
     for h in range(NH):
         for k in range(1, ND):
-            l_copy(h, k, (dom + ND - k) % ND).wait_recv()
-    for h in range(NH):
-        for k in range(1, ND):
             l_copy(h, k, dom).wait_send()
-        w_copy(h, 0, dom, side_peer).wait_send()
-        w_copy(h, 1, dom, chip_peer).wait_send()
-        w_copy(h, 2, side_dom, chip_peer).wait_send()
 
 
 def update_kernel(weights, inverse, rows, num, temps, edge, evid, out, evid_out, staged, sems):
@@ -532,8 +620,8 @@
     temp = 3.0 / math.sqrt(band)
     bounds = jnp.stack([tilt_low, tilt_high])
 
-    schedule = plan(width // LANES, 13, 7, 10)
-    line = timeline(schedule, (9.0, 6.0, 9.0, 8.0, 4.0))
+    schedule = plan(width // LANES, CUTS, RANKS)
+    line = timeline(schedule, LAGS)
     count = 1 + max(s["sem"] for s in schedule[0])
     total = NX * NY * NZ * ND * local
     half = total // NH
@@ -564,7 +652,9 @@
             pltpu.VMEM((total, LANES), bf16),
             pltpu.VMEM((refs, half), bf16),
             pltpu.VMEM((NH * 2 * ND, refs, LANES), f32),
-            pltpu.VMEM((ND - 1, NH * 2, refs, LANES), f32),
+            pltpu.VMEM((NH * 2 * ND, refs, LANES), f32),
+            pltpu.VMEM((NH * 2, refs, LANES), f32),
+            pltpu.VMEM((NH, ND, 2, refs, LANES), f32),
             pltpu.VMEM((NH, 8, LANES), f32),
             pltpu.VMEM((NH, 8, LANES), f32),
             pltpu.VMEM((NH, NZ, 8, LANES), f32),
@@ -572,30 +662,31 @@
             pltpu.VMEM((3, refs, LANES), bf16),
             dma(()),
             dma(()),
-            dma((ND,)),
-            dma((ND,)),
+            dma((ND - 1,)),
+            dma((ND - 1,)),
             dma((NH,)),
             dma((count,)),
             dma((NH * 2 * ND,)),
-            dma((ND - 1, NH * 2)),
+            dma((NH * 2 * ND,)),
+            dma((NH * 2,)),
             dma((NH, NZ)),
             dma((NH, NZ)),
             dma((NH, NX * NY)),
             dma((NH, NX * NY)),
-            dma((NH, 3)),
-            dma((NH, 3)),
+            dma((NH, 3, 2)),
+            dma((NH, 3, 2)),
             dma((NH, ND)),
             dma((NH, ND)),
         ],
         compiler_params=pltpu.CompilerParams(
-            collective_id=0, has_side_effects=True, vmem_limit_bytes=12 * 1024 * 1024
+            collective_id=0, has_side_effects=True, vmem_limit_bytes=18 * 1024 * 1024
         ),
     )(
         pltpu.with_memory_space_constraint(particles, pltpu.HBM),
         bounds,
         pltpu.with_memory_space_constraint(templates, pltpu.HBM),
     )
-    tile = 256
+    tile = 1024
     updated, evidence = pl.pallas_call(
         update_kernel,
         out_shape=(
@@ -605,7 +696,7 @@
         in_specs=[vmem] * 7,
         out_specs=(pl.BlockSpec(memory_space=pltpu.HBM), vmem),
         scratch_shapes=[pltpu.VMEM((2, refs, 2, tile), f32), dma((2,))],
-        compiler_params=pltpu.CompilerParams(vmem_limit_bytes=8 * 1024 * 1024),
+        compiler_params=pltpu.CompilerParams(vmem_limit_bytes=12 * 1024 * 1024),
     )(weights, inverse, rows, num, temps, edge, evidence)
     evidence = evidence[:, :, :2].reshape(NH, ND, 2, NX, NY, 2, local)
     dom = lax.axis_index("dom")

time: 130 us -> 125 us (0.962)
  Pallas kernels: 128 us -> 122 us
    pallas_call x1, Pallas kernels: 121 us -> 117 us  [on_device(): pl.pallas_call(functools.partial(em_kernel, schedule[0], line, temp), out...]
    pallas_call x1, Pallas kernels: 6.6 us -> 4.99 us  [on_device(): pl.pallas_call(update_kernel, out_shape=(jax.ShapeDtypeStruct((refs, 2, q...]
where the time goes in v4:
time: 125 us
  Pallas kernels  122 us (98%)
    pallas_call x1, Pallas kernels, on_device(): pl.pallas_call(functools.partial(em_kernel, schedule[0], line, temp), out...  117 us
    pallas_call x1, Pallas kernels, on_device(): pl.pallas_call(update_kernel, out_shape=(jax.ShapeDtypeStruct((refs, 2, q...  4.99 us

profile of v4, /device:TPU:1, one launch (start us, length us, event | category | flops | bytes accessed | tf_op | source)
XLA Modules:
  0.0 124.8 jit_solution(11637020106006845146)
XLA Ops:
  0.6 0.7 pad_add_fusion.bounds
  1.3 117.5 %shard_map.59 = (bf16[2048,4096]{1,0:T(8,128)(2,1)S(1)}, bf16[256,4096]{1,0:T(8,128)(2,1)S(1)}, bf16[256,128]{1,0:T(8,128)(2,1)S(1)}, f32[256,4096]{1,0:T(8,128)...) custom-call(bf16[8,2,8192]{2,1,0:T(2,128)(2,1)} %whole_particles.1, ...), custom_call_target="tpu_custom_call" | custom-call | tf_op jit(solution)/shard_map/pallas_call | solution.py:631
  118.8 5.0 %shard_map.60 = (f32[256,2,2048]{2,1,0:T(2,128)}, f32[2,4,8,128]{3,2,1,0:T(8,128)S(1)}) custom-call(bf16[256,1024]{1,0:T(8,128)(2,1)S(1)} %get-tuple-element.11.weights, f32[256,128]{1,0:T(8,128)S(1)} %get-tuple-element.12.inverse, bf16[2048,4096]{1,0:T(8,128)(2,1)S(1)} %get-tuple-element.13.rows, f32[256,4096]{1,0:T(8,128)S(1)} %get-tuple-element.14.num, ...), custom_call_target="tpu_custom_call" | custom-call | tf_op jit(solution)/shard_map/pallas_call | solution.py:690
  123.8 0.2 reshape.12
  124.2 0.7 reshape.13
  (3 shorter events, 0.1 us)

commit v5 on v4

--- a/solution.py
+++ b/solution.py
@@ -13,11 +13,11 @@
 LANES = 128
 RING = (0, 7, 1, 6, 2, 5, 3, 4)
 LINKS = ("x", "y+", "y-", "z+", "z-")
-LATENCY = 3.75
+LATENCY = 4.25
 TILE = 0.0879
 AHEAD = 2.0
-CUTS = ((13, 8, 14), (13, 8, 9))
-RANKS = (3, 2, 2, 3, 0)
+CUTS = ((13, 9, 11), (13, 8, 10))
+RANKS = (3, 0, 2, 3, 0)
 LAGS = (2.5, 11.0, 9.0)
 PREPARE_AT, PREPARE_STEP, PREPARE_PARTS = 6.0, 3.0, 8
 BATCH = 128
@@ -153,7 +153,7 @@
 def em_kernel(
     sends, line, temp, whole_particles, bounds, templates,
     rows, temps, edge, num, weights_1, inverse, evid,
-    particles, split, pairs, masks, weights_0, scores, core_parts, parts, totals, stat_a, stat_b, stat_z, stat_q, power,
+    particles, split, pairs, masks, weights_0, scores, core_parts, parts, totals, stat_a, stat_b, stat_z, stat_q, stat_w, power,
     local_sem, load_sem, a_send, a_recv, send_sem, recv_sem,
     ps_send, pc_recv, px_recv, z_send, z_recv, q_send, q_recv, t_send, t_recv, l_send, l_recv,
 ):
@@ -288,13 +288,13 @@
 
     def core_copy(slot):
         return remote(
-            scores.at[slot], core_parts.at[slot], ps_send.at[slot], pc_recv.at[slot], chip_peer
+            scores.at[slot], core_parts.at[slot], ps_send, pc_recv.at[slot], chip_peer
         )
 
     def side_copy(slot):
         part = slot // (2 * ND) * 2 + slot % 2
         return remote(
-            scores.at[slot], parts.at[part], ps_send.at[slot], px_recv.at[part], side_peer
+            scores.at[slot], parts.at[part], ps_send, px_recv.at[part], side_peer
         )
 
     def combine(slot):
@@ -310,31 +310,21 @@
     def evidence_of(peak, mass):
         return jnp.concatenate([peak, mass, peak, mass], axis=0)
 
-    def stat_copies(h, src, slots, index, peers, ssem, rsem):
-        out = [
-            remote(src.at[h], slots.at[h, index], ssem.at[h, k], rsem.at[h, k], peers[k])
-            for k in range(1, len(peers))
-        ]
-        back = [
-            remote(
-                src.at[h], slots.at[h, (index + len(peers) - k) % len(peers)],
-                ssem.at[h, k], rsem.at[h, k], peers[k],
-            )
-            for k in range(1, len(peers))
-        ]
-        return out, back
-
-    def merged(h, slots):
-        both = slots[h]
+    def send_stats(src, slot, peers, ssem, rsem):
+        for peer in peers:
+            remote(src, slot, ssem, rsem, peer).start()
+
+    def all_but_one(slots, sem):
+        most = slots.at[pl.ds(0, slots.shape[0] - 1)]
+        return pltpu.make_async_copy(most, most, sem)
+
+    def merged(both):
         peak = jnp.max(both[:, :2], axis=0)
         return peak, jnp.sum(both[:, 2:4] * jnp.exp(both[:, :2] - peak[None]), axis=0)
 
-    z_stats = lambda h: stat_copies(h, stat_a, stat_z, z0, z_peer, z_send, z_recv)
-    q_stats = lambda h: stat_copies(h, stat_b, stat_q, q0, q_peer, q_send, q_recv)
-
     def total_copy(h, n, k, owner, peer):
         ref = totals.at[h, owner, k]
-        return remote(ref, ref, t_send.at[h, n, k], t_recv.at[h, n, k], peer)
+        return remote(ref, ref, t_send.at[h], t_recv.at[h, n, k], peer)
 
     def sum_scores(h):
         peaks, masses = [], []
@@ -349,37 +339,50 @@
         tile = evidence_of(jnp.concatenate(peaks, axis=0), jnp.concatenate(masses, axis=0))
         stat_a[h] = tile
         stat_z[h, z0] = tile
-        for c in z_stats(h)[0]:
-            c.start()
+        send_stats(stat_a.at[h], stat_z.at[h, z0], z_peer[1:], z_send.at[h], z_recv.at[h])
         total_copy(h, 0, 0, dom, side_peer).start()
         for k in range(2):
             total_copy(h, 1, k, dom, chip_peer).start()
 
     def merge_z(h):
-        for c in z_stats(h)[1]:
-            c.wait_recv()
-        tile = evidence_of(*merged(h, stat_z))
+        all_but_one(stat_z.at[h], z_recv.at[h]).wait()
+        tile = evidence_of(*merged(stat_z[h]))
         stat_b[h] = tile
-        stat_q[h, q0] = tile
-        for c in q_stats(h)[0]:
-            c.start()
+        if h == 0:
+            stat_q[q0] = tile
+            send_stats(stat_b.at[0], stat_q.at[q0], q_peer[1:], q_send.at[0], q_recv.at[0])
+        else:
+            slot = dom * NX * NY + q0
+            stat_w[slot] = tile
+            wide = [
+                dict(q_peer[n % (NX * NY)], **d_peer[n // (NX * NY)])
+                for n in range(1, ND * NX * NY)
+            ]
+            send_stats(stat_b.at[1], stat_w.at[slot], wide, q_send.at[1], q_recv.at[1])
         total_copy(h, 0, 1, dom, side_peer).start()
 
     weights = (weights_0, weights_1)
 
-    def l_copy(h, k, owner):
-        ref = evid.at[h, owner]
-        return remote(ref, ref, l_send.at[h, k], l_recv.at[h, k], d_peer[k])
-
-    def weigh(h):
-        for c in q_stats(h)[1]:
-            c.wait_recv()
-        peak, mass = merged(h, stat_q)
+    def l_copy(k, owner):
+        ref = evid.at[0, owner]
+        return remote(ref, ref, l_send.at[k], l_recv.at[k], d_peer[k])
+
+    def weigh_first():
+        all_but_one(stat_q, q_recv.at[0]).wait()
+        peak, mass = merged(stat_q[...])
         log_evidence = peak + jnp.log(mass)
-        evid[h, dom] = evidence_of(log_evidence, mass)
+        evid[0, dom] = evidence_of(log_evidence, mass)
         for k in range(1, ND):
-            l_copy(h, k, dom).start()
-        fill_weights(h, dom, log_evidence)
+            l_copy(k, dom).start()
+        fill_weights(0, dom, log_evidence)
+
+    def weigh_second():
+        all_but_one(stat_w, q_recv.at[1]).wait()
+        for owner in range(ND):
+            peak, mass = merged(stat_w[owner * NX * NY : (owner + 1) * NX * NY])
+            log_evidence = peak + jnp.log(mass)
+            evid[1, owner] = evidence_of(log_evidence, mass)
+            fill_weights(1, owner, log_evidence)
 
     def fill_weights(h, owner, log_evidence):
         for k in range(2):
@@ -397,11 +400,11 @@
             total_copy(h, 1, k, chip_dom, chip_peer).wait_recv()
             total_copy(h, 2, k, diag_dom, chip_peer).wait_recv()
 
-    def fill_others(h):
+    def fill_others():
         for k in range(1, ND):
             owner = (dom + ND - k) % ND
-            l_copy(h, k, owner).wait_recv()
-            fill_weights(h, owner, evid[h, owner][:2])
+            l_copy(k, owner).wait_recv()
+            fill_weights(0, owner, evid[0, owner][:2])
 
     def first_numerator(piece):
         columns = pl.ds(piece * quarter, quarter)
@@ -529,10 +532,10 @@
     combine_last(1)
     forward(0)
     sum_scores(1)
-    weigh(0)
+    weigh_first()
     receive(0)
     merge_z(1)
-    fill_others(0)
+    fill_others()
     first_numerator(0)
     forward(1)
     for h in range(NH):
@@ -542,33 +545,24 @@
         pltpu.make_async_copy(every, every, send_sem.at[h]).wait()
     first_numerator(1)
     receive(1)
-    weigh(1)
-
-    def drain(slot, carry):
-        @pl.when(owner_of(slot) != dom)
-        def _():
-            core_copy(slot).wait_send()
-
-        return carry
-
-    lax.fori_loop(0, NH * 2 * ND, drain, 0)
+    den = jnp.dot(weights_0[...], masks[:half], preferred_element_type=jnp.float32)
+    inverse[...] = den
+
     for k in range(ND - 1):
         a_copy(k, dom, others[k][0]).wait_send()
+    sent = scores.at[pl.ds(0, (NH * 2 * ND) * 3 // 4)]
+    pltpu.make_async_copy(sent, sent, ps_send).wait()
     for h in range(NH):
-        for c in z_stats(h)[0] + q_stats(h)[0]:
-            c.wait_send()
-        for k in range(2):
-            total_copy(h, 0, k, dom, side_peer).wait_send()
-            total_copy(h, 1, k, dom, chip_peer).wait_send()
-            total_copy(h, 2, k, side_dom, chip_peer).wait_send()
-    den = jnp.dot(weights_0[...], masks[:half], preferred_element_type=jnp.float32)
-    inverse[...] = den
-    fill_others(1)
+        all_but_one(stat_z.at[h], z_send.at[h]).wait()
+        sent = totals.at[h, pl.ds(0, 3)]
+        pltpu.make_async_copy(sent, sent, t_send.at[h]).wait()
+    all_but_one(stat_q, q_send.at[0]).wait()
+    for k in range(1, ND):
+        l_copy(k, dom).wait_send()
+    weigh_second()
     den = inverse[...] + jnp.dot(weights_1[...], masks[half:], preferred_element_type=jnp.float32)
     inverse[...] = 1.0 / (den + 1.0)
-    for h in range(NH):
-        for k in range(1, ND):
-            l_copy(h, k, dom).wait_send()
+    all_but_one(stat_w, q_send.at[1]).wait()
 
 
 def update_kernel(weights, inverse, rows, num, temps, edge, evid, out, evid_out, staged, sems):
@@ -658,7 +652,8 @@
             pltpu.VMEM((NH, 8, LANES), f32),
             pltpu.VMEM((NH, 8, LANES), f32),
             pltpu.VMEM((NH, NZ, 8, LANES), f32),
-            pltpu.VMEM((NH, NX * NY, 8, LANES), f32),
+            pltpu.VMEM((NX * NY, 8, LANES), f32),
+            pltpu.VMEM((ND * NX * NY, 8, LANES), f32),
             pltpu.VMEM((3, refs, LANES), bf16),
             dma(()),
             dma(()),
@@ -666,17 +661,17 @@
             dma((ND - 1,)),
             dma((NH,)),
             dma((count,)),
-            dma((NH * 2 * ND,)),
+            dma(()),
             dma((NH * 2 * ND,)),
             dma((NH * 2,)),
-            dma((NH, NZ)),
-            dma((NH, NZ)),
-            dma((NH, NX * NY)),
-            dma((NH, NX * NY)),
+            dma((NH,)),
+            dma((NH,)),
+            dma((NH,)),
+            dma((NH,)),
+            dma((NH,)),
             dma((NH, 3, 2)),
-            dma((NH, 3, 2)),
-            dma((NH, ND)),
-            dma((NH, ND)),
+            dma((ND,)),
+            dma((ND,)),
         ],
         compiler_params=pltpu.CompilerParams(
             collective_id=0, has_side_effects=True, vmem_limit_bytes=18 * 1024 * 1024

time: 125 us -> 117 us (0.936)
  Pallas kernels: 122 us -> 115 us
    pallas_call x1, Pallas kernels: 117 us -> 110 us  [on_device(): pl.pallas_call(functools.partial(em_kernel, schedule[0], line, temp), out...]
where the time goes in v5:
time: 117 us
  Pallas kernels  115 us (98%)
    pallas_call x1, Pallas kernels, on_device(): pl.pallas_call(functools.partial(em_kernel, schedule[0], line, temp), out...  110 us
    pallas_call x1, Pallas kernels, on_device(): pl.pallas_call(update_kernel, out_shape=(jax.ShapeDtypeStruct((refs, 2, q...  5 us

profile of v5, /device:TPU:1, one launch (start us, length us, event | category | flops | bytes accessed | tf_op | source)
XLA Modules:
  0.0 117.3 jit_solution(13608799825529159527)
XLA Ops:
  0.6 0.7 pad_add_fusion.bounds
  1.3 110.0 %shard_map.59 = (bf16[2048,4096]{1,0:T(8,128)(2,1)S(1)}, bf16[256,4096]{1,0:T(8,128)(2,1)S(1)}, bf16[256,128]{1,0:T(8,128)(2,1)S(1)}, f32[256,4096]{1,0:T(8,128)...) custom-call(bf16[8,2,8192]{2,1,0:T(2,128)(2,1)} %whole_particles.1, ...), custom_call_target="tpu_custom_call" | custom-call | tf_op jit(solution)/shard_map/pallas_call | solution.py:625
  111.3 5.0 %shard_map.60 = (f32[256,2,2048]{2,1,0:T(2,128)}, f32[2,4,8,128]{3,2,1,0:T(8,128)S(1)}) custom-call(bf16[256,1024]{1,0:T(8,128)(2,1)S(1)} %get-tuple-element.11.weights, f32[256,128]{1,0:T(8,128)S(1)} %get-tuple-element.12.inverse, bf16[2048,4096]{1,0:T(8,128)(2,1)S(1)} %get-tuple-element.13.rows, f32[256,4096]{1,0:T(8,128)S(1)} %get-tuple-element.14.num, ...), custom_call_target="tpu_custom_call" | custom-call | tf_op jit(solution)/shard_map/pallas_call | solution.py:685
  116.3 0.2 reshape.12
  116.7 0.7 reshape.13
  (3 shorter events, 0.1 us)

commit v6 on v5

--- a/solution.py
+++ b/solution.py
@@ -151,10 +151,10 @@
 
 
 def em_kernel(
-    sends, line, temp, whole_particles, bounds, templates,
+    sends, line, temp, whole_particles, whole_low, whole_high, templates,
     rows, temps, edge, num, weights_1, inverse, evid,
-    particles, split, pairs, masks, weights_0, scores, core_parts, parts, totals, stat_a, stat_b, stat_z, stat_q, stat_w, power,
-    local_sem, load_sem, a_send, a_recv, send_sem, recv_sem,
+    particles, tilt_low, tilt_high, split, pairs, masks, weights_0, scores, core_parts, parts, totals, stat_a, stat_b, stat_z, stat_q, stat_w, power,
+    local_sem, load_sem, tilt_sem, a_send, a_recv, send_sem, recv_sem,
     ps_send, pc_recv, px_recv, z_send, z_recv, q_send, q_recv, t_send, t_recv, l_send, l_recv,
 ):
     segments, batches, late = line
@@ -190,6 +190,12 @@
     )
     fetch = pltpu.make_async_copy(whole_particles, particles, local_sem)
     fetch.start()
+    limits = [
+        pltpu.make_async_copy(src, dst, tilt_sem.at[n])
+        for n, (src, dst) in enumerate(((whole_low, tilt_low), (whole_high, tilt_high)))
+    ]
+    for c in limits:
+        c.start()
     load.start()
     barrier = pltpu.get_barrier_semaphore()
     greeted = list(target.values()) + d_peer[1:]
@@ -221,9 +227,11 @@
     local = particles.shape[0]
     item = lax.broadcasted_iota(jnp.int32, (local, 1), 0)
     low, high = jnp.zeros((local, 1), jnp.float32), jnp.zeros((local, 1), jnp.float32)
+    for c in limits:
+        c.wait()
     for n in range(local):
-        low = jnp.where(item == n, bounds[0, n].astype(jnp.float32), low)
-        high = jnp.where(item == n, bounds[1, n].astype(jnp.float32), high)
+        low = jnp.where(item == n, tilt_low[n].astype(jnp.float32), low)
+        high = jnp.where(item == n, tilt_high[n].astype(jnp.float32), high)
     column = lax.broadcasted_iota(jnp.int32, (local, quarter), 1)
     bins = (column * 37 % NBIN).astype(jnp.float32)
     seen = (low <= bins) & (bins < high)
@@ -530,13 +538,13 @@
     for step in late:
         chain[step[1]](0)
     combine_last(1)
+    weigh_first()
     forward(0)
     sum_scores(1)
-    weigh_first()
     receive(0)
-    merge_z(1)
     fill_others()
     first_numerator(0)
+    merge_z(1)
     forward(1)
     for h in range(NH):
         sent = sum((s["hi"] - s["lo"]) * UNIT for s in sends if s["unit"][0] == h)
@@ -569,7 +577,28 @@
     refs, width = num.shape
     quarter, half = width // 2, weights.shape[1]
     tile = staged.shape[3]
-    evid_out[...] = evid[...]
+
+    dom = lax.axis_index("dom")
+    source = evid[dom // 2]
+    lane = lax.broadcasted_iota(jnp.int32, (ND, LANES), 1)
+    row = lax.broadcasted_iota(jnp.int32, (ND, LANES), 0)
+    local = LANES // 16
+    mine = (lane // (LANES // ND) == row) & (lane // local % 2 == dom % 2)
+    spread = []
+    for z in range(NZ):
+        values = jnp.broadcast_to(source[z % ND, z // ND : z // ND + 1], (ND, LANES))
+        spread.append(jnp.where(mine, values, 0.0))
+    spread = jnp.concatenate(spread, axis=1)
+    at = lax.broadcasted_iota(jnp.int32, (NZ * LANES, LANES), 0)
+    to = lax.broadcasted_iota(jnp.int32, (NZ * LANES, LANES), 1)
+    goal = at % LANES // 16 % 2 * (LANES // 2) + at // LANES * local + at % local
+    place = jnp.where(goal == to, 1.0, 0.0).astype(jnp.bfloat16)
+    moved_parts = []
+    for _ in range(3):
+        head = spread.astype(jnp.bfloat16)
+        spread = spread - head.astype(jnp.float32)
+        moved_parts.append(jnp.dot(head, place, preferred_element_type=jnp.float32))
+    evid_out[...] = moved_parts[0] + (moved_parts[1] + moved_parts[2])
 
     def copy(j):
         columns = pl.ds(pl.multiple_of(j * tile, tile), tile)
@@ -612,8 +641,6 @@
     quarter = band // ND
     width = 2 * quarter
     temp = 3.0 / math.sqrt(band)
-    bounds = jnp.stack([tilt_low, tilt_high])
-
     schedule = plan(width // LANES, CUTS, RANKS)
     line = timeline(schedule, LAGS)
     count = 1 + max(s["sem"] for s in schedule[0])
@@ -633,14 +660,12 @@
             jax.ShapeDtypeStruct((refs, LANES), f32),
             jax.ShapeDtypeStruct((NH, ND, 8, LANES), f32),
         ),
-        in_specs=[
-            pl.BlockSpec(memory_space=pltpu.HBM),
-            pl.BlockSpec(memory_space=pltpu.SMEM),
-            pl.BlockSpec(memory_space=pltpu.HBM),
-        ],
+        in_specs=[pl.BlockSpec(memory_space=pltpu.HBM)] * 4,
         out_specs=(vmem,) * 7,
         scratch_shapes=[
             pltpu.VMEM(particles.shape, bf16),
+            pltpu.SMEM((local,), jnp.int32),
+            pltpu.SMEM((local,), jnp.int32),
             pltpu.VMEM((ND * local, width), bf16),
             pltpu.VMEM((refs, 2, quarter), bf16),
             pltpu.VMEM((total, LANES), bf16),
@@ -657,6 +682,7 @@
             pltpu.VMEM((3, refs, LANES), bf16),
             dma(()),
             dma(()),
+            dma((2,)),
             dma((ND - 1,)),
             dma((ND - 1,)),
             dma((NH,)),
@@ -677,28 +703,24 @@
             collective_id=0, has_side_effects=True, vmem_limit_bytes=18 * 1024 * 1024
         ),
     )(
-        pltpu.with_memory_space_constraint(particles, pltpu.HBM),
-        bounds,
-        pltpu.with_memory_space_constraint(templates, pltpu.HBM),
+        *(
+            pltpu.with_memory_space_constraint(a, pltpu.HBM)
+            for a in (particles, tilt_low, tilt_high, templates)
+        )
     )
     tile = 1024
     updated, evidence = pl.pallas_call(
         update_kernel,
         out_shape=(
             jax.ShapeDtypeStruct((refs, 2, quarter), f32),
-            jax.ShapeDtypeStruct(evidence.shape, f32),
+            jax.ShapeDtypeStruct((ND, LANES), f32),
         ),
         in_specs=[vmem] * 7,
         out_specs=(pl.BlockSpec(memory_space=pltpu.HBM), vmem),
         scratch_shapes=[pltpu.VMEM((2, refs, 2, tile), f32), dma((2,))],
         compiler_params=pltpu.CompilerParams(vmem_limit_bytes=12 * 1024 * 1024),
     )(weights, inverse, rows, num, temps, edge, evidence)
-    evidence = evidence[:, :, :2].reshape(NH, ND, 2, NX, NY, 2, local)
-    dom = lax.axis_index("dom")
-    evidence = lax.dynamic_index_in_dim(evidence, dom // 2, 0, keepdims=False)
-    evidence = lax.dynamic_index_in_dim(evidence, dom % 2, 4, keepdims=False)
-    evidence = jnp.transpose(evidence, (2, 3, 1, 0, 4)).reshape(-1)
-    return updated, evidence
+    return updated, evidence.reshape(-1)
 
 
 def solution(mesh):

time: 117 us -> 116 us (level)
  no operation moved by 1% of the time
where the time goes in v6:
time: 116 us
  Pallas kernels  115 us (99%)
    pallas_call x1, Pallas kernels, on_device(): pl.pallas_call(functools.partial(em_kernel, schedule[0], line, temp), out...  110 us
    pallas_call x1, Pallas kernels, on_device(): pl.pallas_call(update_kernel, out_shape=(jax.ShapeDtypeStruct((refs, 2, q...  5.91 us

profile of v6, /device:TPU:1, one launch (start us, length us, event | category | flops | bytes accessed | tf_op | source)
XLA Modules:
  0.0 116.3 jit_solution(7786507174529752960)
XLA Ops:
  0.6 109.6 %shard_map.59 = (bf16[2048,4096]{1,0:T(8,128)(2,1)S(1)}, bf16[256,4096]{1,0:T(8,128)(2,1)S(1)}, bf16[256,128]{1,0:T(8,128)(2,1)S(1)}, f32[256,4096]{1,0:T(8,128)...) custom-call(bf16[8,2,8192]{2,1,0:T(2,128)(2,1)} %whole_particles.1, ...), custom_call_target="tpu_custom_call" | custom-call | tf_op jit(solution)/shard_map/pallas_call | solution.py:652
  110.2 5.9 %shard_map.60 = (f32[256,2,2048]{2,1,0:T(2,128)}, f32[4,128]{1,0:T(4,128)}) custom-call(bf16[256,1024]{1,0:T(8,128)(2,1)S(1)} %get-tuple-element.11.weights, f32[256,128]{1,0:T(8,128)S(1)} %get-tuple-element.12.inverse, bf16[2048,4096]{1,0:T(8,128)(2,1)S(1)} %get-tuple-element.13.rows, f32[256,4096]{1,0:T(8,128)S(1)} %get-tuple-element.14.num, ...), custom_call_target="tpu_custom_call" | custom-call | tf_op jit(solution)/shard_map/pallas_call | solution.py:712

commit v7 on v6

--- a/solution.py
+++ b/solution.py
@@ -348,8 +348,8 @@
         stat_a[h] = tile
         stat_z[h, z0] = tile
         send_stats(stat_a.at[h], stat_z.at[h, z0], z_peer[1:], z_send.at[h], z_recv.at[h])
-        total_copy(h, 0, 0, dom, side_peer).start()
         for k in range(2):
+            total_copy(h, 0, k, dom, side_peer).start()
             total_copy(h, 1, k, dom, chip_peer).start()
 
     def merge_z(h):
@@ -367,7 +367,6 @@
                 for n in range(1, ND * NX * NY)
             ]
             send_stats(stat_b.at[1], stat_w.at[slot], wide, q_send.at[1], q_recv.at[1])
-        total_copy(h, 0, 1, dom, side_peer).start()
 
     weights = (weights_0, weights_1)
 
@@ -497,6 +496,11 @@
                         copy_of(s, s["unit"]).start()
                 for w in wanted:
                     hear(w)
+
+        @pl.when((phase > 0) & (phase != last_of[0] + 1))
+        def _():
+            for slot in slots_of(phase - 1):
+                combine(slot)
 
         slots = slots_of(phase)
         heres = [pl.ds(pl.multiple_of(slot * BATCH, BATCH), BATCH) for slot in slots]
@@ -526,11 +530,6 @@
             def _(slot=slot):
                 core_copy(slot).start()
 
-        @pl.when((phase > 0) & (phase != last_of[0] + 1))
-        def _():
-            for slot in slots_of(phase - 1):
-                combine(slot)
-
         return carry
 
     lax.fori_loop(0, len(segments), phase_body, 0)
@@ -578,12 +577,44 @@
     quarter, half = width // 2, weights.shape[1]
     tile = staged.shape[3]
 
+    def copy(j):
+        columns = pl.ds(pl.multiple_of(j * tile, tile), tile)
+        return pltpu.make_async_copy(staged.at[j % 2], out.at[:, :, columns], sems.at[j % 2])
+
+    lane = lax.broadcasted_iota(jnp.int32, (refs, LANES), 1)
+    stash = (lane == LOW_AT) | (lane == HIGH_AT)
+    scale = jnp.concatenate([inverse[...]] * (tile // LANES), axis=1)
+
+    def step(j, carry):
+        @pl.when(j >= 2)
+        def _():
+            copy(j - 2).wait()
+
+        for c in range(2):
+            columns = pl.ds(pl.multiple_of(c * quarter + j * tile, tile), tile)
+            total = num[:, columns] + jnp.dot(
+                weights[...], rows[half:, columns], preferred_element_type=jnp.float32
+            )
+            staged[j % 2, :, c, :] = (total + temps[:, columns].astype(jnp.float32)) * scale
+
+        @pl.when(j == 0)
+        def _():
+            first = staged[0, :, 0, :LANES]
+            kept = edge[...].astype(jnp.float32) * inverse[...]
+            staged[0, :, 0, :LANES] = jnp.where(stash, kept, first)
+
+        copy(j).start()
+        return carry
+
+    steps = quarter // tile
+    lax.fori_loop(0, steps, step, 0)
+
     dom = lax.axis_index("dom")
     source = evid[dom // 2]
-    lane = lax.broadcasted_iota(jnp.int32, (ND, LANES), 1)
+    lanes = lax.broadcasted_iota(jnp.int32, (ND, LANES), 1)
     row = lax.broadcasted_iota(jnp.int32, (ND, LANES), 0)
     local = LANES // 16
-    mine = (lane // (LANES // ND) == row) & (lane // local % 2 == dom % 2)
+    mine = (lanes // (LANES // ND) == row) & (lanes // local % 2 == dom % 2)
     spread = []
     for z in range(NZ):
         values = jnp.broadcast_to(source[z % ND, z // ND : z // ND + 1], (ND, LANES))
@@ -599,38 +630,6 @@
         spread = spread - head.astype(jnp.float32)
         moved_parts.append(jnp.dot(head, place, preferred_element_type=jnp.float32))
     evid_out[...] = moved_parts[0] + (moved_parts[1] + moved_parts[2])
-
-    def copy(j):
-        columns = pl.ds(pl.multiple_of(j * tile, tile), tile)
-        return pltpu.make_async_copy(staged.at[j % 2], out.at[:, :, columns], sems.at[j % 2])
-
-    lane = lax.broadcasted_iota(jnp.int32, (refs, LANES), 1)
-    stash = (lane == LOW_AT) | (lane == HIGH_AT)
-    scale = jnp.concatenate([inverse[...]] * (tile // LANES), axis=1)
-
-    def step(j, carry):
-        @pl.when(j >= 2)
-        def _():
-            copy(j - 2).wait()
-
-        for c in range(2):
-            columns = pl.ds(pl.multiple_of(c * quarter + j * tile, tile), tile)
-            total = num[:, columns] + jnp.dot(
-                weights[...], rows[half:, columns], preferred_element_type=jnp.float32
-            )
-            staged[j % 2, :, c, :] = (total + temps[:, columns].astype(jnp.float32)) * scale
-
-        @pl.when(j == 0)
-        def _():
-            first = staged[0, :, 0, :LANES]
-            kept = edge[...].astype(jnp.float32) * inverse[...]
-            staged[0, :, 0, :LANES] = jnp.where(stash, kept, first)
-
-        copy(j).start()
-        return carry
-
-    steps = quarter // tile
-    lax.fori_loop(0, steps, step, 0)
     copy(steps - 2).wait()
     copy(steps - 1).wait()
 

time: 116 us -> 116 us (level)
  no operation moved by 1% of the time
where the time goes in v7:
time: 116 us
  Pallas kernels  115 us (99%)
    pallas_call x1, Pallas kernels, on_device(): pl.pallas_call(functools.partial(em_kernel, schedule[0], line, temp), out...  110 us
    pallas_call x1, Pallas kernels, on_device(): pl.pallas_call(update_kernel, out_shape=(jax.ShapeDtypeStruct((refs, 2, q...  5.43 us

profile of v7, /device:TPU:1, one launch (start us, length us, event | category | flops | bytes accessed | tf_op | source)
XLA Modules:
  0.0 115.9 jit_solution(17792321052698066203)
XLA Ops:
  0.6 109.7 %shard_map.59 = (bf16[2048,4096]{1,0:T(8,128)(2,1)S(1)}, bf16[256,4096]{1,0:T(8,128)(2,1)S(1)}, bf16[256,128]{1,0:T(8,128)(2,1)S(1)}, f32[256,4096]{1,0:T(8,128)...) custom-call(bf16[8,2,8192]{2,1,0:T(2,128)(2,1)} %whole_particles.1, ...), custom_call_target="tpu_custom_call" | custom-call | tf_op jit(solution)/shard_map/pallas_call | solution.py:651
  110.3 5.4 %shard_map.60 = (f32[256,2,2048]{2,1,0:T(2,128)}, f32[4,128]{1,0:T(4,128)}) custom-call(bf16[256,1024]{1,0:T(8,128)(2,1)S(1)} %get-tuple-element.11.weights, f32[256,128]{1,0:T(8,128)S(1)} %get-tuple-element.12.inverse, bf16[2048,4096]{1,0:T(8,128)(2,1)S(1)} %get-tuple-element.13.rows, f32[256,4096]{1,0:T(8,128)S(1)} %get-tuple-element.14.num, ...), custom_call_target="tpu_custom_call" | custom-call | tf_op jit(solution)/shard_map/pallas_call | solution.py:711
